TPU v7x, 32 devices: a whole 2x2x4 slice. The times are simulated.
32 devices in a mesh: dp: 16 (over z, y, core), tensor: 2 (over x).
Axes of the slice: x: 2, y: 2, z: 4, core: 2. Of those that a mesh axis runs over, the one named last changes fastest.
Arguments:
- tokens: float32 [2, 25600, 512], P(None, ('dp', 'tensor')), may hold values from -6 to 6
- key_mask: int32 [2, 128, 200], P(None, 'dp'), may hold values from 0 to 1, as said below
- expert_ids: int32 [2, 25600, 2], P(None, 'dp'), may hold values from 0 to 31, as said below
- slot_ids: int32 [2, 25600, 2], P(None, 'dp'), may hold values from -1 to 119, as said below
- norm1_gain: float32 [512], P(('dp', 'tensor')), may hold values from 0.25 to 1.75
- norm1_bias: float32 [512], P(('dp', 'tensor')), may hold values from -3 to 3
- qkv_weight: bfloat16 [512, 3, 512], P('dp', None, 'tensor'), may hold values from -0.25 to 0.25
- out_weight: bfloat16 [512, 512], P('tensor', 'dp'), may hold values from -1 to 1
- norm2_gain: float32 [512], P(('dp', 'tensor')), may hold values from 0.25 to 1.75
- norm2_bias: float32 [512], P(('dp', 'tensor')), may hold values from -3 to 3
- router_weight: float32 [512, 32], P(('dp', 'tensor')), may hold values from -0.25 to 0.25
- expert_in: bfloat16 [32, 512, 2048], P(None, 'dp', 'tensor'), may hold values from -0.25 to 0.25
- expert_out: bfloat16 [32, 2048, 512], P(None, 'tensor', 'dp'), may hold values from -3 to 3
- cotangent: float32 [2, 25600, 512], P(None, ('dp', 'tensor')), may hold values from -6 to 6
Outputs:
- block_out: float32 [2, 25600, 512], P(None, ('dp', 'tensor'))
- input_grad: float32 [2, 25600, 512], P(None, ('dp', 'tensor'))
- norm1_gain_grad: float32 [512], P(('dp', 'tensor'))
- norm1_bias_grad: float32 [512], P(('dp', 'tensor'))
- qkv_grad: float32 [512, 3, 512], P('dp', None, 'tensor')
- out_grad: float32 [512, 512], P('tensor', 'dp')
- norm2_gain_grad: float32 [512], P(('dp', 'tensor'))
- norm2_bias_grad: float32 [512], P(('dp', 'tensor'))
- router_grad: float32 [512, 32], P(('dp', 'tensor'))
- expert_in_grad: float32 [32, 512, 2048], P(None, 'dp', 'tensor')
- expert_out_grad: float32 [32, 2048, 512], P(None, 'tensor', 'dp')
Inputs may be any that keep to these rules, and one draw needn't show every extreme that they name: `key_mask`: position 0 of every image is 1; positions 197 to 199 are 0. `expert_ids`: each row names two different experts. `slot_ids`: slots count within routing groups of 1600 consecutive rows of a micro-batch. -1 marks a dropped route; no two other routes of a group share expert and slot, and the slots used by one expert in a group are 0, 1, 2, ... without gaps.
All inputs are finite; a program needn't handle non-finite values.
Results may differ from a plain program's by a relative error of at most 0.035.
Values may be sent and summed in bfloat16 or wider, within the bound.
A program may use at most 264 MiB of HBM per device.

v0:
```python
import jax
import jax.numpy as jnp
from jax import lax
from jax.sharding import PartitionSpec as P

HEAD = 64
CAP = 120


EPSILON = 1e-06
FIRST_DIMS = (((0,), (0,)), ((), ()))
LAST_DIMS = (((1,), (1,)), ((), ()))


def norm_rows(values, gain, offset):
    center = jnp.mean(values, -1, keepdims=True)
    shifted = values - center
    spread = jnp.mean(shifted * shifted, -1, keepdims=True)
    return shifted * lax.rsqrt(spread + EPSILON) * gain + offset


def slot_table(routes, slot_count):
    places = lax.broadcasted_iota(jnp.int32, (routes.shape[0], slot_count), 1)
    hits = (routes[:, 0:1] == places) | (routes[:, 1:2] == places)
    return hits.astype(jnp.bfloat16)


def per_device(
    tokens,
    key_mask,
    expert_ids,
    slot_ids,
    norm1_gain,
    norm1_bias,
    qkv_weight,
    out_weight,
    norm2_gain,
    norm2_bias,
    router_weight,
    expert_in,
    expert_out,
    cotangent,
):
    highest = lax.Precision.HIGHEST
    gain_one, bias_one, gain_two, bias_two, router_full = (
        lax.all_gather(norm1_gain, ("dp", "tensor"), axis=0, tiled=True),
        lax.all_gather(norm1_bias, ("dp", "tensor"), axis=0, tiled=True),
        lax.all_gather(norm2_gain, ("dp", "tensor"), axis=0, tiled=True),
        lax.all_gather(norm2_bias, ("dp", "tensor"), axis=0, tiled=True),
        lax.all_gather(router_weight, ("dp", "tensor"), axis=0, tiled=True),
    )
    micro_count, own_rows, model_width = tokens.shape
    image_count, seq_length = (key_mask.shape[1], key_mask.shape[2])
    group_rows = image_count * seq_length
    expert_count = expert_in.shape[0]
    hidden_width = expert_in.shape[2]
    slot_count = expert_count * CAP
    head_width = qkv_weight.shape[2]
    local_heads = head_width // HEAD
    scaling = HEAD ** (-0.5)
    own_start = lax.axis_index("tensor") * own_rows

    def fetch_attention():
        qkv_full, attn_full = (
            lax.all_gather(qkv_weight, "dp", axis=0, tiled=True),
            lax.all_gather(out_weight, "dp", axis=1, tiled=True),
        )
        qkv_every, attn_every = (None, None)
        return (qkv_full.reshape(model_width, 3 * head_width), attn_full, qkv_every, attn_every)

    def current_weights():
        return (
            fetch_attention(),
            (
                lax.all_gather(expert_in, "dp", axis=1, tiled=True),
                lax.all_gather(expert_out, "dp", axis=2, tiled=True),
            ),
        )

    qkv_acc = jnp.zeros((model_width, 3 * head_width), jnp.float32)
    attn_acc = jnp.zeros((head_width, model_width), jnp.float32)
    first_acc = jnp.zeros((expert_count, model_width, hidden_width), jnp.float32)
    second_acc = jnp.zeros((expert_count, hidden_width, model_width), jnp.float32)
    router_acc = jnp.zeros((model_width, expert_count), jnp.float32)
    gain_one_acc = jnp.zeros((model_width,), jnp.float32)
    bias_one_acc = jnp.zeros((model_width,), jnp.float32)
    gain_two_acc = jnp.zeros((model_width,), jnp.float32)
    bias_two_acc = jnp.zeros((model_width,), jnp.float32)
    block_list = []
    grad_list = []
    for micro_step in range(micro_count):
        row_block = tokens[micro_step]
        cot_block = cotangent[micro_step]
        key_flags = key_mask[micro_step]
        experts = expert_ids[micro_step]
        places = slot_ids[micro_step]
        retained = (places >= 0).astype(jnp.float32)
        slot_index = jnp.where(places >= 0, experts * CAP + places, slot_count)

        def masked_scores(query, keyed):
            raw = (
                jnp.einsum("bqhd,bkhd->bhqk", query, keyed, preferred_element_type=jnp.float32)
                * scaling
            )
            return jnp.where(key_flags[:, None, None, :] > 0, raw, -1e30)

        (qkv_joined, attn_local, qkv_every, attn_every), (first_layer, second_layer) = (
            current_weights()
        )
        normed_own = norm_rows(row_block, gain_one, bias_one).astype(jnp.bfloat16)
        normed_all = lax.all_gather(normed_own, "tensor", axis=0, tiled=True)
        projected = jnp.dot(normed_all, qkv_joined, preferred_element_type=jnp.float32).astype(
            jnp.bfloat16
        )
        projected = projected.reshape(image_count, seq_length, 3, local_heads, HEAD)
        query, keyed, valued = (projected[:, :, 0], projected[:, :, 1], projected[:, :, 2])
        scores = masked_scores(query, keyed)
        row_max = jnp.max(scores, -1, keepdims=True)
        lifted = jnp.exp(scores - row_max)
        row_total = jnp.sum(lifted, -1, keepdims=True)
        probs = lifted / row_total
        log_total = row_max + jnp.log(row_total)
        mixed = jnp.einsum(
            "bhqk,bkhd->bqhd",
            probs.astype(jnp.bfloat16),
            valued,
            preferred_element_type=jnp.float32,
        )
        mixed = mixed.astype(jnp.bfloat16).reshape(group_rows, head_width)
        middle = row_block + lax.psum_scatter(
            jnp.dot(mixed, attn_local, preferred_element_type=jnp.float32).astype(jnp.bfloat16),
            "tensor",
            scatter_dimension=0,
            tiled=True,
        ).astype(jnp.float32)
        routed_own = norm_rows(middle, gain_two, bias_two).astype(jnp.bfloat16)
        piece = lax.all_gather(routed_own, "tensor", axis=0, tiled=True)
        count = piece.shape[0]
        gates = jax.nn.softmax(
            jnp.dot(piece.astype(jnp.float32), router_full, precision=highest), axis=-1
        )
        picks = lax.broadcasted_iota(jnp.int32, (count, 2, expert_count), 2) == experts[:, :, None]
        picked_gates = jnp.sum(jnp.where(picks, gates[:, None, :], 0.0), -1) * retained
        chosen = picked_gates
        table = slot_table(slot_index, slot_count)
        dispatched = lax.dot_general(table, piece, FIRST_DIMS, preferred_element_type=jnp.float32)
        dispatched, chosen = (dispatched, chosen)
        slot_gate = (
            jnp.zeros((slot_count + 1,), jnp.float32)
            .at[slot_index.reshape(-1)]
            .set(chosen.reshape(-1))[:slot_count]
        )
        dispatched_low = dispatched.astype(jnp.bfloat16).reshape(expert_count, CAP, model_width)
        hidden_pre = jnp.einsum(
            "ecd,edf->ecf", dispatched_low, first_layer, preferred_element_type=jnp.float32
        )
        hidden = jax.nn.gelu(hidden_pre).astype(jnp.bfloat16)
        expert_part = jnp.einsum(
            "ecf,efd->ecd", hidden, second_layer, preferred_element_type=jnp.float32
        ).reshape(slot_count, model_width)
        weighted = jnp.concatenate(
            [slot_gate[:, None] * expert_part, jnp.zeros((1, model_width), jnp.float32)], 0
        )
        block_list.append(
            middle
            + lax.psum_scatter(
                (weighted[slot_index[:, 0]] + weighted[slot_index[:, 1]]).astype(jnp.bfloat16),
                "tensor",
                scatter_dimension=0,
                tiled=True,
            ).astype(jnp.float32)
        )
        (qkv_joined, attn_local, qkv_every, attn_every), (first_layer, second_layer) = (
            current_weights()
        )
        cot_low = cot_block.astype(jnp.bfloat16)
        picked_grads = lax.dot_general(
            slot_table(slot_index, slot_count),
            lax.all_gather(cot_low, "tensor", axis=0, tiled=True),
            FIRST_DIMS,
            preferred_element_type=jnp.float32,
        )
        gate_part = jnp.sum(picked_grads * expert_part, -1)
        result_grad = (
            (slot_gate[:, None] * picked_grads)
            .astype(jnp.bfloat16)
            .reshape(expert_count, CAP, model_width)
        )
        hidden_grad = jnp.einsum(
            "ecd,efd->ecf", result_grad, second_layer, preferred_element_type=jnp.float32
        )
        pre_grad = jax.vjp(jax.nn.gelu, hidden_pre)[1](hidden_grad)[0].astype(jnp.bfloat16)
        first_acc = first_acc + jnp.einsum(
            "ecd,ecf->edf", dispatched_low, pre_grad, preferred_element_type=jnp.float32
        )
        second_acc = second_acc + jnp.einsum(
            "ecf,ecd->efd", hidden, result_grad, preferred_element_type=jnp.float32
        )
        dispatch_grad = jnp.einsum(
            "ecf,edf->ecd", pre_grad, first_layer, preferred_element_type=jnp.float32
        ).reshape(slot_count, model_width)
        dispatch_grad = jnp.concatenate(
            [dispatch_grad, jnp.zeros((1, model_width), jnp.float32)], 0
        )
        gate_padded = jnp.concatenate([gate_part, jnp.zeros((1,), jnp.float32)], 0)
        row_grads = dispatch_grad[slot_index[:, 0]] + dispatch_grad[slot_index[:, 1]]
        gate_grads = gate_padded[slot_index]
        own_row_grads, own_gate_grads = (
            lax.psum_scatter(
                row_grads.astype(jnp.bfloat16), "tensor", scatter_dimension=0, tiled=True
            ).astype(jnp.float32),
            lax.psum_scatter(
                gate_grads.astype(jnp.bfloat16), "tensor", scatter_dimension=0, tiled=True
            ).astype(jnp.float32),
        )
        own_experts = lax.dynamic_slice_in_dim(experts, own_start, own_rows, 0)
        routed_wide = routed_own.astype(jnp.float32)
        own_gates = jax.nn.softmax(jnp.dot(routed_wide, router_full, precision=highest), axis=-1)
        own_picks = (
            lax.broadcasted_iota(jnp.int32, (own_rows, 2, expert_count), 2)
            == own_experts[:, :, None]
        )
        gate_cot = jnp.sum(jnp.where(own_picks, own_gate_grads[:, :, None], 0.0), 1)
        logit_grad = own_gates * (gate_cot - jnp.sum(own_gates * gate_cot, -1, keepdims=True))
        routed_grad = own_row_grads + jnp.dot(logit_grad, router_full.T, precision=highest)
        router_acc = router_acc + jnp.dot(routed_wide.T, logit_grad, precision=highest)
        middle_part, gain_step, bias_step = jax.vjp(norm_rows, middle, gain_two, bias_two)[1](
            routed_grad
        )
        gain_two_acc = gain_two_acc + gain_step
        bias_two_acc = bias_two_acc + bias_step
        middle_grad = cot_block + middle_part
        attn_cot = lax.all_gather(middle_grad.astype(jnp.bfloat16), "tensor", axis=0, tiled=True)
        attn_acc = attn_acc + lax.dot_general(
            mixed, attn_cot, FIRST_DIMS, preferred_element_type=jnp.float32
        )
        mixed_grad = lax.dot_general(
            attn_cot, attn_local, LAST_DIMS, preferred_element_type=jnp.float32
        )
        mixed_grad = mixed_grad.astype(jnp.bfloat16).reshape(
            image_count, seq_length, local_heads, HEAD
        )
        again_probs = jnp.exp(masked_scores(query, keyed) - log_total)
        prob_grad = jnp.einsum(
            "bqhd,bkhd->bhqk", mixed_grad, valued, preferred_element_type=jnp.float32
        )
        value_grad = jnp.einsum(
            "bhqk,bqhd->bkhd",
            again_probs.astype(jnp.bfloat16),
            mixed_grad,
            preferred_element_type=jnp.float32,
        ).astype(jnp.bfloat16)
        inner_sum = jnp.sum(again_probs * prob_grad, -1, keepdims=True)
        score_grad = (again_probs * (prob_grad - inner_sum)).astype(jnp.bfloat16)
        query_grad = (
            jnp.einsum("bhqk,bkhd->bqhd", score_grad, keyed, preferred_element_type=jnp.float32)
            * scaling
        ).astype(jnp.bfloat16)
        keyed_grad = (
            jnp.einsum("bhqk,bqhd->bkhd", score_grad, query, preferred_element_type=jnp.float32)
            * scaling
        ).astype(jnp.bfloat16)
        proj_grad = jnp.stack([query_grad, keyed_grad, value_grad], 2).reshape(
            group_rows, 3 * head_width
        )
        qkv_acc = qkv_acc + lax.dot_general(
            normed_all, proj_grad, FIRST_DIMS, preferred_element_type=jnp.float32
        )
        normed_grad = lax.psum_scatter(
            lax.dot_general(
                proj_grad, qkv_joined, LAST_DIMS, preferred_element_type=jnp.float32
            ).astype(jnp.bfloat16),
            "tensor",
            scatter_dimension=0,
            tiled=True,
        ).astype(jnp.float32)
        input_part, gain_step, bias_step = jax.vjp(norm_rows, row_block, gain_one, bias_one)[1](
            normed_grad
        )
        gain_one_acc = gain_one_acc + gain_step
        bias_one_acc = bias_one_acc + bias_step
        grad_list.append(middle_grad + input_part)
    qkv_grad, out_grad, first_grad, second_grad = (
        lax.psum_scatter(
            qkv_acc.reshape(model_width, 3, head_width).astype(jnp.bfloat16),
            "dp",
            scatter_dimension=0,
            tiled=True,
        ).astype(jnp.float32),
        lax.psum_scatter(
            attn_acc.astype(jnp.bfloat16), "dp", scatter_dimension=1, tiled=True
        ).astype(jnp.float32),
        lax.psum_scatter(
            first_acc.astype(jnp.bfloat16), "dp", scatter_dimension=1, tiled=True
        ).astype(jnp.float32),
        lax.psum_scatter(
            second_acc.astype(jnp.bfloat16), "dp", scatter_dimension=2, tiled=True
        ).astype(jnp.float32),
    )
    gain_one_grad, bias_one_grad, gain_two_grad, bias_two_grad, router_grad = (
        lax.psum_scatter(gain_one_acc, ("dp", "tensor"), scatter_dimension=0, tiled=True),
        lax.psum_scatter(bias_one_acc, ("dp", "tensor"), scatter_dimension=0, tiled=True),
        lax.psum_scatter(gain_two_acc, ("dp", "tensor"), scatter_dimension=0, tiled=True),
        lax.psum_scatter(bias_two_acc, ("dp", "tensor"), scatter_dimension=0, tiled=True),
        lax.psum_scatter(router_acc, ("dp", "tensor"), scatter_dimension=0, tiled=True),
    )
    return (
        jnp.stack(block_list),
        jnp.stack(grad_list),
        gain_one_grad,
        bias_one_grad,
        qkv_grad,
        out_grad,
        gain_two_grad,
        bias_two_grad,
        router_grad,
        first_grad,
        second_grad,
    )


def solution(mesh):
    placed = (
        P(None, ("dp", "tensor"), None),
        P(None, "dp", None),
        P(None, "dp", None),
        P(None, "dp", None),
        P(("dp", "tensor")),
        P(("dp", "tensor")),
        P("dp", None, "tensor"),
        P("tensor", "dp"),
        P(("dp", "tensor")),
        P(("dp", "tensor")),
        P(("dp", "tensor"), None),
        P(None, "dp", "tensor"),
        P(None, "tensor", "dp"),
        P(None, ("dp", "tensor"), None),
    )
    return jax.shard_map(
        per_device,
        mesh=mesh,
        in_specs=placed,
        out_specs=(
            P(None, ("dp", "tensor"), None),
            P(None, ("dp", "tensor"), None),
            P(("dp", "tensor")),
            P(("dp", "tensor")),
            P("dp", None, "tensor"),
            P("tensor", "dp"),
            P(("dp", "tensor")),
            P(("dp", "tensor")),
            P(("dp", "tensor"), None),
            P(None, "dp", "tensor"),
            P(None, "tensor", "dp"),
        ),
        check_vma=False,
    )
```

profile of v0, /device:TPU:4, one launch (start us, length us, event | category | flops | bytes accessed | tf_op | source)
XLA Modules:
  0.0 2145.7 jit_solution(1419710168144649038)
XLA Ops:
  12.3 41.3 %all-reduce.14 = (f32[512]{0:T(512)S(1)}, f32[512]{0:T(512)S(1)}, f32[512]{0:T(512)S(1)}, f32[512]{0:T(512)S(1)}) all-reduce(f32[512]{0:T(512)S(1)} %dynamic-update-slice.1, f32[512]{0:T(512)S(1)} %dynamic-update-slice, f32[512]{0:T(512)S(1)} %dynamic-update-slice.3, ...), channel_id=1, replica_groups=mesh['dp'=16,'tensor'=2] {'dp','tensor'}, use_global_device_ids=true, to_apply=%add.5 | all-reduce | flops 2048 | bytes 16384
  56.1 17.7 all_gather.67
  73.9 25.4 %all_gather.66 = bf16[512,3,256]{2,0,1:T(8,128)(2,1)} all-gather(bf16[32,3,256]{2,0,1:T(8,128)(2,1)} %param.20), channel_id=1, replica_groups=mesh['dp'=16,'tensor'=2] {'dp'}, dimensions={0}, use_global_device_ids=true | all-gather | bytes 835584 | tf_op jit(solution)/shard_map/all_gather | solution.py:65
  189.3 24.3 %reduce-scatter.23.cloned.1.call-done = bf16[800,512]{1,0:T(8,128)(2,1)} async-done(((bf16[1600,512]{1,0:T(8,128)(2,1)}), bf16[800,512]{1,0:T(8,128)(2,1)}) %reduce-scatter.23.cloned.1.call-update) | async-done | bytes 819216 | tf_op jit(solution)/shard_map/reduce_scatter | solution.py:130
  227.1 61.9 %all_gather.71 = f32[512,32]{1,0:T(8,128)S(1)} all-gather(f32[16,32]{1,0:T(8,128)S(1)} %copy-done.106), channel_id=1, replica_groups=mesh['dp'=16,'tensor'=2] {'dp','tensor'}, dimensions={0}, use_global_device_ids=true | all-gather | bytes 67584 | tf_op jit(solution)/shard_map/all_gather | solution.py:50
  301.7 16.4 scatter_custom_fusion
  318.1 16.2 scatter_custom_fusion.1
  355.7 94.7 %all-gather.15.cloned.1.call-done = bf16[32,512,1024]{2,1,0:T(8,128)(2,1)} async-done(((bf16[32,32,1024]{2,1,0:T(8,128)(2,1)}), bf16[32,512,1024]{2,1,0:T(8,128)(2,1)}) %all-gather.15.cloned.1.call-update) | async-done | bytes 33554448 | tf_op jit(solution)/shard_map/all_gather | solution.py:75
  450.3 21.0 fusion.145
  471.3 148.6 %all-gather.17.cloned.1.call-done = bf16[32,1024,512]{1,2,0:T(8,128)(2,1)} async-done(((bf16[32,1024,32]{1,2,0:T(8,128)(2,1)}), bf16[32,1024,512]{1,2,0:T(8,128)(2,1)}) %all-gather.17.cloned.1.call-update) | async-done | bytes 33554448 | tf_op jit(solution)/shard_map/all_gather | solution.py:76
  620.0 23.2 %fusion.130 = f32[32,120,512]{2,1,0:T(8,128)} fusion(bf16[32,1024,512]{1,2,0:T(8,128)(2,1)} %all-gather.17.cloned.1.call-done, f32[32,120,1024]{2,1,0:T(8,128)} %fusion.145), kind=kOutput, calls=%fused_computation.282 | convolution fusion | flops 4061921280 | bytes 57147392 | tf_op jit(solution)/shard_map/ecf,efd->ecd/dot_general | solution.py:158
  650.4 17.7 fusion.32
  668.1 19.2 gather_fusion.9
  689.0 20.8 fusion.144
  709.8 22.2 %fusion.129 = f32[32,120,512]{2,1,0:T(8,128)} fusion(bf16[32,1024,512]{1,2,0:T(8,128)(2,1)} %all-gather.17.cloned.1.call-done, f32[32,120,1024]{2,1,0:T(8,128)} %fusion.144), kind=kOutput, calls=%fused_computation.281 | convolution fusion | flops 4061921280 | bytes 57147392 | tf_op jit(solution)/shard_map/ecf,efd->ecd/dot_general | solution.py:158
  732.0 16.6 fusion.33
  750.5 24.5 %fusion.16 = bf16[32,120,1024]{2,1,0:T(8,128)(2,1)} fusion(f32[32,120,1024]{2,1,0:T(8,128)} %fusion.144, bf16[32,120,512]{2,1,0:T(8,128)(2,1)S(1)} %bitcast.286, bf16[32,1024,512]{1,2,0:T(8,128)(2,1)} %all-gather.17.cloned.1.call-done), kind=kOutput, calls=%fused_computation.34 | convolution fusion | flops 4105175040 | bytes 61079552 | tf_op jit(solution)/shard_map/ecd,efd->ecf/dot_general | solution.py:189
  775.1 21.0 fusion.146
  796.1 19.2 gather_fusion.6
  846.6 24.1 %fusion.23 = bf16[32,120,1024]{2,1,0:T(8,128)(2,1)} fusion(f32[32,120,1024]{2,1,0:T(8,128)} %fusion.145, bf16[32,120,512]{2,1,0:T(8,128)(2,1)} %bitcast.288, bf16[32,1024,512]{1,2,0:T(8,128)(2,1)} %all-gather.17.cloned.1.call-done), kind=kOutput, calls=%fused_computation.41 | convolution fusion | flops 4105175040 | bytes 61079552 | tf_op jit(solution)/shard_map/ecd,efd->ecf/dot_general | solution.py:189
  870.6 21.0 fusion.147
  1018.6 27.3 %all-gather.25.cloned.1.call-done = bf16[1600,512]{1,0:T(8,128)(2,1)} async-done(((bf16[800,512]{1,0:T(8,128)(2,1)}), bf16[1600,512]{1,0:T(8,128)(2,1)}) %all-gather.25.cloned.1.call-update) | async-done | bytes 1638416 | tf_op jit(solution)/shard_map/all_gather | solution.py:233
  1138.3 30.2 %fusion.128 = f32[32,1024,512]{1,2,0:T(8,128)} fusion(bf16[32,120,512]{2,1,0:T(8,128)(2,1)} %bitcast.287, f32[32,120,1024]{2,1,0:T(8,128)} %fusion.144), kind=kOutput, calls=%fused_computation.280 | convolution fusion | flops 4061921280 | bytes 86769664 | tf_op jit(solution)/shard_map/ecf,ecd->efd/dot_general | solution.py:196
  1171.2 40.5 %add_convert_fusion = bf16[32,1024,512]{1,2,0:T(8,128)(2,1)} fusion(f32[32,1024,512]{1,2,0:T(8,128)} %fusion.128, bf16[32,120,512]{2,1,0:T(8,128)(2,1)} %bitcast.289, f32[32,120,1024]{2,1,0:T(8,128)} %fusion.145), kind=kOutput, calls=%fused_computation.12 | convolution fusion | flops 4095475712 | bytes 120324096 | tf_op jit(solution)/shard_map/ecf,ecd->efd/dot_general | solution.py:196
  1211.8 27.6 %fusion.150 = f32[32,512,1024]{2,1,0:T(8,128)} fusion(bf16[32,120,512]{2,1,0:T(8,128)(2,1)} %bitcast.285, bf16[32,120,1024]{2,1,0:T(8,128)(2,1)} %fusion.16), kind=kOutput, calls=%fused_computation.302 | convolution fusion | flops 4026531840 | bytes 78905344 | tf_op jit(solution)/shard_map/ecd,ecf->edf/dot_general | solution.py:193
  1239.5 37.4 %add_convert_fusion.1 = bf16[32,512,1024]{2,1,0:T(8,128)(2,1)} fusion(f32[32,512,1024]{2,1,0:T(8,128)} %fusion.150, bf16[32,120,512]{2,1,0:T(8,128)(2,1)} %bitcast.283, bf16[32,120,1024]{2,1,0:T(8,128)(2,1)} %fusion.23), kind=kOutput, calls=%fused_computation.13 | convolution fusion | flops 4060086272 | bytes 112459776 | tf_op jit(solution)/shard_map/ecd,ecf->edf/dot_general | solution.py:193
  1289.0 21.2 reduce-scatter.29.cloned.1.call-done
  1310.2 29.7 %reduce-scatter.33.cloned.1.call-done = bf16[800,512]{1,0:T(8,128)(2,1)} async-done(((bf16[1600,512]{1,0:T(8,128)(2,1)}), bf16[800,512]{1,0:T(8,128)(2,1)}) %reduce-scatter.33.cloned.1.call-update) | async-done | bytes 819216 | tf_op jit(solution)/shard_map/reduce_scatter | solution.py:269
  1344.3 40.2 %all-reduce.13 = (f32[512]{0:T(512)S(1)}, f32[512]{0:T(512)S(1)}, f32[512]{0:T(512)S(1)}, f32[512]{0:T(512)S(1)}) all-reduce(f32[512]{0:T(512)S(1)} %add.372, f32[512]{0:T(512)S(1)} %add.373, f32[512]{0:T(512)S(1)} %add.376, f32[512]{0:T(512)S(1)} %add.377), channel_id=12, replica_groups=mesh['dp'=16,'tensor'=2] {'dp','tensor'}, use_global_device_ids=true, to_apply=%region_52.53.clone | all-reduce | flops 2048 | bytes 16384
  1394.5 280.2 %reduce-scatter.41.cloned.1.call-done = bf16[32,1024,32]{1,2,0:T(8,128)(2,1)} async-done(((bf16[32,1024,512]{1,2,0:T(8,128)(2,1)}), bf16[32,1024,32]{1,2,0:T(8,128)(2,1)}) %reduce-scatter.41.cloned.1.call-update) | async-done | bytes 2097168 | tf_op jit(solution)/shard_map/reduce_scatter | solution.py:296
  1678.8 329.7 %reduce-scatter.39.cloned.1.call-done = bf16[32,32,1024]{2,1,0:T(8,128)(2,1)} async-done(((bf16[32,512,1024]{2,1,0:T(8,128)(2,1)}), bf16[32,32,1024]{2,1,0:T(8,128)(2,1)}) %reduce-scatter.39.cloned.1.call-update) | async-done | bytes 2097168 | tf_op jit(solution)/shard_map/reduce_scatter | solution.py:293
  2012.6 126.4 %reduce-scatter.37.cloned.1.call-done = f32[16,32]{1,0:T(8,128)} async-done(((f32[512,32]{1,0:T(8,128)}), f32[16,32]{1,0:T(8,128)}) %reduce-scatter.37.cloned.1.call-update) | async-done | bytes 2064 | tf_op jit(solution)/shard_map/reduce_scatter | solution.py:305
  (497 shorter events, 441.4 us)
Async XLA Ops:
  7.2 94.3 %all-gather.11.cloned.1.call-start = ((), (), s32[]{:S(2)}) async-start(), calls=%async_computation.14 | async-start | bytes 2457600 | tf_op jit(solution)/shard_map/all_gather | solution.py:111
  53.6 164.2 %copy-start.99 = (f32[512]{0:T(512)}, f32[512]{0:T(512)S(1)}, u32[]{:S(2)}) copy-start(f32[512]{0:T(512)S(1)} %get-tuple-element.101) | copy-start | bytes 6148
  55.3 90.2 %all-gather.19.cloned.1.call-start = ((), (), s32[]{:S(2)}) async-start(), calls=%async_computation.20 | async-start | bytes 2457600 | tf_op jit(solution)/shard_map/all_gather | solution.py:111
  56.1 133.2 %reduce-scatter.19.cloned.1.call-start = ((), (), s32[]{:S(2)}) async-start(), calls=%async_computation.15 | async-start | bytes 2457600 | tf_op jit(solution)/shard_map/reduce_scatter | solution.py:130
  73.9 112.3 %copy-start.27 = (bf16[256,512]{0,1:T(8,128)(2,1)}, bf16[256,512]{0,1:T(8,128)(2,1)S(1)}, u32[]{:S(2)}) copy-start(bf16[256,512]{0,1:T(8,128)(2,1)S(1)} %all_gather.67) | copy-start | bytes 786436
  145.2 68.4 %reduce-scatter.23.cloned.1.call-start = ((), (), s32[]{:S(2)}) async-start(), calls=%async_computation.21 | async-start | bytes 2457600 | tf_op jit(solution)/shard_map/reduce_scatter | solution.py:130
  189.2 104.7 %all-gather.21.cloned.1.call-start = ((), (), s32[]{:S(2)}) async-start(), calls=%async_computation.22 | async-start | bytes 2457600 | tf_op jit(solution)/shard_map/all_gather | solution.py:137
  220.0 76.9 %all-gather.13.cloned.1.call-start = ((), (), s32[]{:S(2)}) async-start(), calls=%async_computation.16 | async-start | bytes 2457600 | tf_op jit(solution)/shard_map/all_gather | solution.py:137
  220.6 229.7 %all-gather.15.cloned.1.call-start = ((), (), s32[]{:S(2)}) async-start(), calls=%async_computation.17 | async-start | bytes 35651584 | tf_op jit(solution)/shard_map/all_gather | solution.py:75
  221.4 398.6 %all-gather.17.cloned.1.call-start = ((), (), s32[]{:S(2)}) async-start(), calls=%async_computation.18 | async-start | bytes 35651584 | tf_op jit(solution)/shard_map/all_gather | solution.py:76
  222.1 428.2 %all-gather.27.cloned.1.call-start = ((), (), s32[]{:S(2)}) async-start(), calls=%async_computation.28 | async-start | bytes 2457600 | tf_op jit(solution)/shard_map/all_gather | solution.py:179
  223.6 508.4 %all-gather.23.cloned.1.call-start = ((), (), s32[]{:S(2)}) async-start(), calls=%async_computation.24 | async-start | bytes 2457600 | tf_op jit(solution)/shard_map/all_gather | solution.py:179
  224.2 766.0 %reduce-scatter.45.cloned.1.call-start = ((), (), s32[]{:S(2)}) async-start(), calls=%async_computation.37 | async-start | bytes 614400
  225.0 109.4 %copy-start.107 = (s32[1600]{0:T(1024)}, s32[1600]{0:T(1024)S(1)}, u32[]{:S(2)}) copy-start(s32[1600]{0:T(1024)S(1)} %get-tuple-element.88) | copy-start | bytes 19204
  225.0 109.4 %copy-start.109 = (s32[1600]{0:T(1024)}, s32[1600]{0:T(1024)S(1)}, u32[]{:S(2)}) copy-start(s32[1600]{0:T(1024)S(1)} %get-tuple-element.89) | copy-start | bytes 19204
  689.0 304.2 %reduce-scatter.43.cloned.1.call-start = ((), (), s32[]{:S(2)}) async-start(), calls=%async_computation.36 | async-start | bytes 614400
  842.8 157.3 %reduce-scatter.27.cloned.1.call-start = ((), (), s32[]{:S(2)}) async-start(), calls=%async_computation.25 | async-start | bytes 2457600 | tf_op jit(solution)/shard_map/reduce_scatter | solution.py:209
  846.5 157.6 %reduce-scatter.31.cloned.1.call-start = ((), (), s32[]{:S(2)}) async-start(), calls=%async_computation.29 | async-start | bytes 2457600 | tf_op jit(solution)/shard_map/reduce_scatter | solution.py:209
  921.3 88.8 %reduce-scatter.25.cloned.1.call-start = ((), (), s32[]{:S(2)}) async-start(), calls=%async_computation.23 | async-start | bytes 2457600 | tf_op jit(solution)/shard_map/reduce_scatter | solution.py:166
  951.5 58.7 %reduce-scatter.21.cloned.1.call-start = ((), (), s32[]{:S(2)}) async-start(), calls=%async_computation.19 | async-start | bytes 2457600 | tf_op jit(solution)/shard_map/reduce_scatter | solution.py:166
  981.4 64.6 %all-gather.25.cloned.1.call-start = ((), (), s32[]{:S(2)}) async-start(), calls=%async_computation.26 | async-start | bytes 2457600 | tf_op jit(solution)/shard_map/all_gather | solution.py:233
  1017.8 58.0 %all-gather.29.cloned.1.call-start = ((), (), s32[]{:S(2)}) async-start(), calls=%async_computation.30 | async-start | bytes 2457600 | tf_op jit(solution)/shard_map/all_gather | solution.py:233
  1018.4 267.7 %all-reduce.17.cloned.1.call-start = ((), (), s32[]{:S(2)}) async-start(), calls=%async_computation.38 | async-start | bytes 2097152
  1129.8 157.8 %reduce-scatter.35.cloned.1.call-start = ((), (), s32[]{:S(2)}) async-start(), calls=%async_computation.32 | async-start | bytes 278528 | tf_op jit(solution)/shard_map/reduce_scatter | solution.py:290
  1133.7 176.5 %reduce-scatter.29.cloned.1.call-start = ((), (), s32[]{:S(2)}) async-start(), calls=%async_computation.27 | async-start | bytes 2457600 | tf_op jit(solution)/shard_map/reduce_scatter | solution.py:269
  1138.3 201.7 %reduce-scatter.33.cloned.1.call-start = ((), (), s32[]{:S(2)}) async-start(), calls=%async_computation.31 | async-start | bytes 2457600 | tf_op jit(solution)/shard_map/reduce_scatter | solution.py:269
  1171.2 503.5 %reduce-scatter.41.cloned.1.call-start = ((), (), s32[]{:S(2)}) async-start(), calls=%async_computation.35 | async-start | bytes 35651584 | tf_op jit(solution)/shard_map/reduce_scatter | solution.py:296
  1211.8 796.7 %reduce-scatter.39.cloned.1.call-start = ((), (), s32[]{:S(2)}) async-start(), calls=%async_computation.34 | async-start | bytes 35651584 | tf_op jit(solution)/shard_map/reduce_scatter | solution.py:293
  1277.0 861.9 %reduce-scatter.37.cloned.1.call-start = ((), (), s32[]{:S(2)}) async-start(), calls=%async_computation.33 | async-start | bytes 270336 | tf_op jit(solution)/shard_map/reduce_scatter | solution.py:305
  1281.9 58.0 %copy-start.3 = (f32[2,800,512]{2,1,0:T(8,128)S(1)}, f32[2,800,512]{2,1,0:T(8,128)}, u32[]{:S(2)}) copy-start(f32[2,800,512]{2,1,0:T(8,128)} %param.14) | copy-start | bytes 9830404
  1281.9 58.0 %copy-start.54 = (f32[800]{0:T(1024)S(1)}, f32[800]{0:T(1024)}, u32[]{:S(2)}) copy-start(f32[800]{0:T(1024)} %copy-done.53) | copy-start | bytes 9604
  1281.9 58.0 %copy-start.56 = (f32[800]{0:T(1024)S(1)}, f32[800]{0:T(1024)}, u32[]{:S(2)}) copy-start(f32[800]{0:T(1024)} %copy-done.55) | copy-start | bytes 9604
  (114 other events, 1188.0 us)
Sparse Core Ops, SparseCore 0:
  55.4 26.9 all-gather.10
  84.5 27.9 all-gather.18
  145.3 24.1 reduce-scatter.18
  189.3 24.2 reduce-scatter.22
  220.1 29.8 all-gather.20
  251.4 29.6 all-gather.12
  282.7 167.5 all-gather.14
  451.9 168.0 all-gather.16
  622.1 28.2 all-gather.26
  651.8 27.9 all-gather.22
  689.1 13.3 reduce-scatter.44
  842.9 13.3 reduce-scatter.42
  858.6 26.8 reduce-scatter.26
  921.5 26.8 reduce-scatter.30
  951.6 26.8 reduce-scatter.24
  981.5 26.9 reduce-scatter.20
  1018.0 27.9 all-gather.24
  1047.9 27.9 all-gather.28
  1129.9 93.5 all-reduce.16
  1226.9 54.9 reduce-scatter.34
  1284.2 25.9 reduce-scatter.28
  1313.0 26.8 reduce-scatter.32
  1344.2 330.5 reduce-scatter.40
  1678.8 329.6 reduce-scatter.38
  2011.3 127.6 reduce-scatter.36
where the time goes:
time: 2160 us; the launch traced here: 2150 us
  waiting for transfers between devices  1100 us (51%)
  matrix products  465 us (22%)
  local copies, waits for them, and re-layouts  293 us (14%)
  blocking collectives  186 us (9%)
  other arithmetic  82.1 us (4%)
    reduce_scatter x1, waiting for transfers between devices, per_device(): lax.psum_scatter(first_acc.astype(jnp.bfloat16), 'dp', scatter_dimension=...  330 us
    reduce_scatter x1, waiting for transfers between devices, per_device(): lax.psum_scatter(second_acc.astype(jnp.bfloat16), 'dp', scatter_dimension...  280 us
    all_gather x1, waiting for transfers between devices, current_weights(): lax.all_gather(expert_out, 'dp', axis=2, tiled=True)  149 us
    reduce_scatter x1, waiting for transfers between devices, per_device(): lax.psum_scatter(router_acc, ('dp', 'tensor'), scatter_dimension=0, tiled...  126 us
    all_gather x1, waiting for transfers between devices, current_weights(): lax.all_gather(expert_in, 'dp', axis=1, tiled=True)  94.7 us
    unnamed x2, blocking collectives  81.5 us
    dot_general x2, matrix products, per_device(): jnp.einsum('ecf,ecd->efd', hidden, result_grad, preferred_element_type=jn...  70.7 us
    dot_general x2, matrix products, per_device(): jnp.einsum('ecd,ecf->edf', dispatched_low, pre_grad, preferred_element_ty...  65 us
  transfers between devices with their start and end apart: 25, of which 11 were waited for; matrix products, arithmetic and copies ran while one was open for 35% of the time, Pallas kernels for 0%

commit v1 on v0

v1 whole, which is shorter than its diff:
```python
import functools

import jax
import jax.numpy as jnp
from jax import lax
from jax.experimental import pallas as pl
from jax.experimental.pallas import tpu as pltpu
from jax.sharding import Mesh, PartitionSpec as P

HEAD = 64
CAP = 120
EPSILON = 1e-06
LANES = 128
VMEM = 60 * 1024 * 1024
NN = (((1,), (0,)), ((), ()))
NT = (((1,), (1,)), ((), ()))
TN = (((0,), (0,)), ((), ()))
HIGH = lax.Precision.HIGHEST
GELU_C = 0.7978845608028654
GELU_A = 0.044715


def mm(a, b, dims=NN, precision=None):
    return lax.dot_general(a, b, dims, precision=precision, preferred_element_type=jnp.float32)


def three_parts(value):
    high = value.astype(jnp.bfloat16)
    rest = value - high.astype(jnp.float32)
    middle = rest.astype(jnp.bfloat16)
    last = (rest - middle.astype(jnp.float32)).astype(jnp.bfloat16)
    return high, middle, last


def standardize(values):
    center = jnp.mean(values, -1, keepdims=True)
    shifted = values - center
    spread = jnp.mean(shifted * shifted, -1, keepdims=True)
    inverse = lax.rsqrt(spread + EPSILON)
    return shifted * inverse, inverse


def norm_back(grad, unit, inverse):
    return inverse * (
        grad
        - jnp.mean(grad, -1, keepdims=True)
        - unit * jnp.mean(grad * unit, -1, keepdims=True)
    )


def even_lanes(shape):
    return lax.broadcasted_iota(jnp.int32, shape, 1) < HEAD


def forward_kernel(
    tok_ref, bias_ref, mats_ref, norms_ref, router_ref,
    middle_ref, routed_ref, proj_ref, mixed_ref, gates_ref,
):
    images, length, width = tok_ref.shape
    rows = images * length
    tok = tok_ref[...].reshape(rows, width)
    unit, _ = standardize(tok)
    normed = (unit * norms_ref[0:1] + norms_ref[1:2]).astype(jnp.bfloat16)
    for c in range(3):
        part = mm(normed, mats_ref[c]).reshape(images, length, width)
        for b in range(images):
            proj_ref[b, :, c * width:(c + 1) * width] = part[b].astype(jnp.bfloat16)
    even = even_lanes((length, LANES))
    scale = jnp.bfloat16(HEAD ** -0.5)
    zero = jnp.zeros((), jnp.bfloat16)
    attended = []
    for b in range(images):
        bias = bias_ref[b]
        pieces = []
        for pair in range(width // LANES):
            lanes = slice(pair * LANES, (pair + 1) * LANES)
            query = proj_ref[b, :, lanes] * scale
            keyed = proj_ref[b, :, width + pair * LANES:width + (pair + 1) * LANES]
            valued = proj_ref[b, :, 2 * width + pair * LANES:2 * width + (pair + 1) * LANES]
            halves = []
            for odd in range(2):
                chosen = jnp.where(even != bool(odd), query, zero)
                scores = mm(chosen, keyed, NT) + bias
                lifted = jnp.exp(scores - jnp.max(scores, -1, keepdims=True))
                probs = lifted * (1.0 / jnp.sum(lifted, -1, keepdims=True))
                halves.append(mm(probs.astype(jnp.bfloat16), valued))
            both = jnp.where(even, halves[0], halves[1])
            mixed_ref[b, :, lanes] = both.astype(jnp.bfloat16)
            pieces.append(both)
        attended.append(jnp.concatenate(pieces, 1))
    joined = jnp.concatenate(attended, 0).astype(jnp.bfloat16)
    middle = tok + mm(joined, mats_ref[3], NT)
    middle_ref[...] = middle.reshape(images, length, width)
    unit, _ = standardize(middle)
    routed = (unit * norms_ref[2:3] + norms_ref[3:4]).astype(jnp.bfloat16)
    wide = routed.astype(jnp.float32)
    routed_ref[...] = wide.reshape(images, length, width).astype(jnp.bfloat16)
    logits = mm(wide, router_ref[...], NN, HIGH)
    lane = lax.broadcasted_iota(jnp.int32, logits.shape, 1)
    logits = jnp.where(lane < 32, logits, -1e30)
    lifted = jnp.exp(logits - jnp.max(logits, -1, keepdims=True))
    gates = lifted / jnp.sum(lifted, -1, keepdims=True)
    gates_ref[...] = gates.reshape(images, length, LANES)


def attention_forward(tok, bias, mats, norms, router, per_step):
    images, length, width = tok.shape

    def rows(last):
        return pl.BlockSpec((per_step, length, last), lambda s: (s, 0, 0))

    def whole(a):
        return pl.BlockSpec(a.shape, lambda s: (0,) * a.ndim)

    shapes = [
        (width, jnp.float32), (width, jnp.bfloat16), (3 * width, jnp.bfloat16),
        (width, jnp.bfloat16), (LANES, jnp.float32),
    ]
    return pl.pallas_call(
        forward_kernel,
        grid=(images // per_step,),
        in_specs=[
            rows(width), pl.BlockSpec((per_step, 1, length), lambda s: (s, 0, 0)),
            whole(mats), whole(norms), whole(router),
        ],
        out_specs=[rows(n) for n, _ in shapes],
        out_shape=[jax.ShapeDtypeStruct((images, length, n), kind) for n, kind in shapes],
        compiler_params=pltpu.CompilerParams(vmem_limit_bytes=VMEM),
        cost_estimate=pl.CostEstimate(
            flops=images * length * width * width * 10, bytes_accessed=images * length * width * 16,
            transcendentals=images * length * length * 8),
        name="attention_forward",
    )(tok, bias, mats, norms, router)


def backward_kernel(
    tok_ref, middle_ref, cot_ref, grad_ref, gates_ref, proj_ref, mixed_ref,
    bias_ref, mats_ref, norms_ref, router_t_ref,
    input_ref, dmats_ref, dnorms_ref, drouter_ref,
    dproj_ref, dmats_acc,
):
    images, length, width = tok_ref.shape
    rows = images * length
    step = pl.program_id(0)

    @pl.when(step == 0)
    def _():
        dmats_acc[...] = jnp.zeros_like(dmats_acc)
        dnorms_ref[...] = jnp.zeros_like(dnorms_ref)
        drouter_ref[...] = jnp.zeros_like(drouter_ref)

    def flat(ref):
        return ref[...].reshape(rows, ref.shape[2])

    middle = flat(middle_ref)
    unit, inverse = standardize(middle)
    grad = flat(grad_ref)
    gates = flat(gates_ref)
    gate_cot = grad[:, width:]
    logit_grad = gates * (gate_cot - jnp.sum(gates * gate_cot, -1, keepdims=True))
    routed = (unit * norms_ref[2:3] + norms_ref[3:4]).astype(jnp.bfloat16)
    drouter_ref[...] += mm(routed.astype(jnp.float32), logit_grad, TN, HIGH)
    routed_grad = grad[:, :width] + mm(logit_grad, router_t_ref[...], NN, HIGH)
    dnorms_ref[2:3] += jnp.sum(routed_grad * unit, 0, keepdims=True)
    dnorms_ref[3:4] += jnp.sum(routed_grad, 0, keepdims=True)
    middle_grad = flat(cot_ref) + norm_back(routed_grad * norms_ref[2:3], unit, inverse)
    attn_cot = middle_grad.astype(jnp.bfloat16)
    joined = jnp.concatenate([mixed_ref[b].astype(jnp.float32) for b in range(images)], 0)
    dmats_acc[3] += mm(attn_cot, joined.astype(jnp.bfloat16), TN)
    mixed_grad = mm(attn_cot, mats_ref[3]).reshape(images, length, width)
    even = even_lanes((length, LANES))
    zero = jnp.zeros((), jnp.bfloat16)
    scale = jnp.bfloat16(HEAD ** -0.5)
    for b in range(images):
        bias = bias_ref[b]
        mixed_low = mixed_grad[b].astype(jnp.bfloat16)
        for pair in range(width // LANES):
            lanes = slice(pair * LANES, (pair + 1) * LANES)
            query = proj_ref[b, :, lanes] * scale
            keyed = proj_ref[b, :, width + pair * LANES:width + (pair + 1) * LANES]
            valued = proj_ref[b, :, 2 * width + pair * LANES:2 * width + (pair + 1) * LANES]
            out_cot = mixed_low[:, lanes]
            query_grad = keyed_grad = value_grad = None
            for odd in range(2):
                mask = even != bool(odd)
                query_half = jnp.where(mask, query, zero)
                keyed_half = jnp.where(mask, keyed, zero)
                cot_half = jnp.where(mask, out_cot, zero)
                scores = mm(query_half, keyed, NT) + bias
                lifted = jnp.exp(scores - jnp.max(scores, -1, keepdims=True))
                probs = lifted * (1.0 / jnp.sum(lifted, -1, keepdims=True))
                prob_grad = mm(cot_half, valued, NT)
                value_part = mm(probs.astype(jnp.bfloat16), cot_half, TN)
                inner = jnp.sum(probs * prob_grad, -1, keepdims=True)
                score_grad = (probs * (prob_grad - inner)).astype(jnp.bfloat16)
                query_part = mm(score_grad, keyed_half)
                keyed_part = mm(score_grad, query_half, TN)
                if odd:
                    query_grad, keyed_grad, value_grad = (
                        query_grad + query_part, keyed_grad + keyed_part, value_grad + value_part)
                else:
                    query_grad, keyed_grad, value_grad = query_part, keyed_part, value_part
            base = pair * LANES
            rows_here = slice(b * length, (b + 1) * length)
            dproj_ref[rows_here, base:base + LANES] = query_grad * (HEAD ** -0.5)
            dproj_ref[rows_here, width + base:width + base + LANES] = keyed_grad
            dproj_ref[rows_here, 2 * width + base:2 * width + base + LANES] = value_grad
    tok = flat(tok_ref)
    unit, inverse = standardize(tok)
    normed = (unit * norms_ref[0:1] + norms_ref[1:2]).astype(jnp.bfloat16)
    normed_grad = jnp.zeros((rows, width), jnp.float32)
    for c in range(3):
        part = dproj_ref[:, c * width:(c + 1) * width].astype(jnp.bfloat16)
        dmats_acc[c] += mm(normed, part, TN)
        normed_grad += mm(part, mats_ref[c], NT)
    dnorms_ref[0:1] += jnp.sum(normed_grad * unit, 0, keepdims=True)
    dnorms_ref[1:2] += jnp.sum(normed_grad, 0, keepdims=True)
    input_grad = middle_grad + norm_back(normed_grad * norms_ref[0:1], unit, inverse)
    input_ref[...] = input_grad.reshape(images, length, width)

    @pl.when(step == pl.num_programs(0) - 1)
    def _():
        dmats_ref[...] = dmats_acc[...].astype(jnp.bfloat16)


def attention_backward(tok, middle, cot, grad, gates, proj, mixed, bias, mats, norms, router_t, per_step):
    images, length, width = tok.shape

    def rows(last):
        return pl.BlockSpec((per_step, length, last), lambda s: (s, 0, 0))

    def whole(shape):
        return pl.BlockSpec(shape, lambda s: (0,) * len(shape))

    return pl.pallas_call(
        backward_kernel,
        grid=(images // per_step,),
        in_specs=[
            rows(width), rows(width), rows(width), rows(width + LANES), rows(LANES),
            rows(3 * width), rows(width), pl.BlockSpec((per_step, 1, length), lambda s: (s, 0, 0)),
            whole(mats.shape), whole(norms.shape), whole(router_t.shape),
        ],
        out_specs=[
            rows(width), whole(mats.shape), whole((4, width)), whole((width, LANES)),
        ],
        out_shape=[
            jax.ShapeDtypeStruct((images, length, width), jnp.float32),
            jax.ShapeDtypeStruct(mats.shape, jnp.bfloat16),
            jax.ShapeDtypeStruct((4, width), jnp.float32),
            jax.ShapeDtypeStruct((width, LANES), jnp.float32),
        ],
        scratch_shapes=[
            pltpu.VMEM((per_step * length, 3 * width), jnp.float32),
            pltpu.VMEM(mats.shape, jnp.float32),
        ],
        compiler_params=pltpu.CompilerParams(vmem_limit_bytes=VMEM),
        cost_estimate=pl.CostEstimate(
            flops=images * length * width * width * 30, bytes_accessed=images * length * width * 30,
            transcendentals=images * length * length * 8),
        name="attention_backward",
    )(tok, middle, cot, grad, gates, proj, mixed, bias, mats, norms, router_t)


def expert_kernel(
    expert_ref, slots_ref, cots_ref, weights_ref, router_ref,
    result_ref, back_ref, dweights_ref,
    rows_t, grads_t, grads, gate_scr, result_acc, back_acc, first_acc, second_acc,
):
    count, width = slots_ref.shape
    tile = weights_ref.shape[-1]
    chunk = rows_t.shape[2]
    step = pl.program_id(0)
    first = weights_ref[:, :, 0, 0].reshape(width, tile)
    second = weights_ref[:, :, 0, 1].reshape(width, tile)

    @pl.when(step == 0)
    def _():
        def prepare(r, carry):
            here = pl.ds(pl.multiple_of(r * chunk, 16), chunk)
            slots = slots_ref[here]
            logits = mm(slots, router_ref[0]) + mm(slots, router_ref[1]) + mm(slots, router_ref[2])
            lane = lax.broadcasted_iota(jnp.int32, logits.shape, 1)
            logits = jnp.where(lane < 32, logits, -1e30)
            lifted = jnp.exp(logits - jnp.max(logits, -1, keepdims=True))
            gates = lifted / jnp.sum(lifted, -1, keepdims=True)
            gate = jnp.sum(jnp.where(lane == expert_ref[0], gates, 0.0), -1, keepdims=True)
            gate_scr[here] = jnp.broadcast_to(gate, logits.shape)
            low = (cots_ref[here].astype(jnp.float32) * gate).astype(jnp.bfloat16)
            grads[here] = low
            rows_t[r] = slots.T
            grads_t[r] = low.T
            result_acc[here] = jnp.zeros((chunk, width), jnp.float32)
            back_acc[here] = jnp.zeros((chunk, width), jnp.float32)
            return carry

        lax.fori_loop(0, count // chunk, prepare, 0)

    first_acc[...] = jnp.zeros_like(first_acc)
    second_acc[...] = jnp.zeros_like(second_acc)

    def work(r, carry):
        here = pl.ds(pl.multiple_of(r * chunk, 16), chunk)
        pre = mm(slots_ref[here], first)
        square = pre * pre
        half = 0.5 + 0.5 * jnp.tanh(pre * (GELU_C + (GELU_C * GELU_A) * square))
        hidden = (pre * half).astype(jnp.bfloat16)
        slope = half + 2.0 * half * (1.0 - half) * pre * (GELU_C + (3.0 * GELU_C * GELU_A) * square)
        hidden_grad = mm(grads[here], second)
        pre_grad = (hidden_grad * slope).astype(jnp.bfloat16)
        result_acc[here] += mm(hidden, second, NT)
        back_acc[here] += mm(pre_grad, first, NT)
        first_acc[...] += mm(rows_t[r], pre_grad)
        second_acc[...] += mm(grads_t[r], hidden)
        return carry

    lax.fori_loop(0, count // chunk, work, 0)
    block = weights_ref.shape[:2] + weights_ref.shape[4:]
    dweights_ref[:, :, 0, 0] = first_acc[...].astype(jnp.bfloat16).reshape(block)
    dweights_ref[:, :, 0, 1] = second_acc[...].astype(jnp.bfloat16).reshape(block)

    @pl.when(step == pl.num_programs(0) - 1)
    def _():
        def finish(r, carry):
            here = pl.ds(pl.multiple_of(r * chunk, 16), chunk)
            result = result_acc[here]
            gate = gate_scr[here][:, 0:1]
            result_ref[here] = (result * gate).astype(jnp.bfloat16)
            gate_grad = jnp.sum(cots_ref[here].astype(jnp.float32) * result, -1, keepdims=True)
            lane = lax.broadcasted_iota(jnp.int32, (chunk, LANES), 1)
            back_ref[here, 0:width] = back_acc[here].astype(jnp.bfloat16)
            back_ref[here, width:width + LANES] = jnp.where(
                lane == expert_ref[0], gate_grad, 0.0).astype(jnp.bfloat16)
            return carry

        lax.fori_loop(0, count // chunk, finish, 0)


def run_expert(expert, slots, cots, weights, router):
    count, width = slots.shape
    planes, inner, parts, _, depth, extent = weights.shape
    tile = min(512, extent)
    per_part = extent // tile
    chunk = 480

    def whole(shape):
        return pl.BlockSpec(shape, lambda s, e: (0,) * len(shape))

    weight_spec = pl.BlockSpec(
        (planes, inner, 1, 2, depth, tile), lambda s, e: (0, 0, s // per_part, 0, 0, s % per_part))
    return pl.pallas_call(
        expert_kernel,
        grid_spec=pltpu.PrefetchScalarGridSpec(
            num_scalar_prefetch=1,
            grid=(parts * per_part,),
            in_specs=[whole(slots.shape), whole(cots.shape), weight_spec, whole(router.shape)],
            out_specs=[whole((count, width)), whole((count, width + LANES)), weight_spec],
            scratch_shapes=[
                pltpu.VMEM((count // chunk, width, chunk), jnp.bfloat16),
                pltpu.VMEM((count // chunk, width, chunk), jnp.bfloat16),
                pltpu.VMEM((count, width), jnp.bfloat16),
                pltpu.VMEM((count, LANES), jnp.float32),
                pltpu.VMEM((count, width), jnp.float32),
                pltpu.VMEM((count, width), jnp.float32),
                pltpu.VMEM((width, tile), jnp.float32),
                pltpu.VMEM((width, tile), jnp.float32),
            ],
        ),
        out_shape=[
            jax.ShapeDtypeStruct((count, width), jnp.bfloat16),
            jax.ShapeDtypeStruct((count, width + LANES), jnp.bfloat16),
            jax.ShapeDtypeStruct(weights.shape, jnp.bfloat16),
        ],
        compiler_params=pltpu.CompilerParams(vmem_limit_bytes=VMEM),
        cost_estimate=pl.CostEstimate(
            flops=12 * count * width * extent * parts,
            bytes_accessed=4 * 2 * width * extent * parts + count * width * 8,
            transcendentals=count * extent * parts),
        name="expert",
    )(expert, slots, cots, weights, router)


def per_device(planes, inner, parts, tokens, key_mask, expert_ids, slot_ids, norm1_gain, norm1_bias,
               qkv_weight, out_weight, norm2_gain, norm2_bias, router_weight, expert_in, expert_out,
               cotangent):
    micros, own_rows, width = tokens.shape
    length = key_mask.shape[2]
    group_rows = own_rows * parts
    images = own_rows // length
    total = micros * images
    experts = expert_in.shape[0]
    homes = inner * parts
    local = experts // homes
    depth, extent = expert_in.shape[1:]
    small = norm1_gain.shape[0]
    every = ("o", "i", "t")
    plane_at, inner_at, part_at = (lax.axis_index(name) for name in every)
    low = jnp.bfloat16

    loose = jnp.concatenate([
        jnp.stack([norm1_gain, norm1_bias, norm2_gain, norm2_bias], 1), router_weight], 1)
    loose_count = 3 * loose.size
    columns = qkv_weight.shape[2]
    loose_rows = -(-loose_count // (16 * columns)) * 16
    loose_low = jnp.concatenate([p.reshape(-1) for p in three_parts(loose)])
    loose_low = jnp.pad(loose_low, (0, loose_rows * columns - loose_count)).reshape(loose_rows, columns)
    packed = jnp.concatenate([
        qkv_weight.transpose(1, 0, 2).reshape(3 * depth, columns), out_weight.T, loose_low], 0)
    gathered = lax.all_gather(packed, ("o", "i"), axis=0)
    gathered = lax.all_gather(gathered, "t", axis=0)
    mats = gathered[:, :, :4 * depth].reshape(parts, planes * inner, 4, depth, columns)
    mats = mats.transpose(2, 1, 3, 0, 4).reshape(4, width, width)
    loose_all = gathered[:, :, 4 * depth:].reshape(parts, planes * inner, loose_rows * columns)
    loose_all = loose_all[:, :, :loose_count].astype(jnp.float32)
    loose_all = loose_all.reshape(parts, planes * inner, 3, small, 4 + experts)
    loose_all = (loose_all[:, :, 0] + loose_all[:, :, 1]) + loose_all[:, :, 2]
    loose_all = loose_all.transpose(1, 0, 2, 3).reshape(width, 4 + experts)
    norms = loose_all[:, :4].T
    router = jnp.pad(loose_all[:, 4:], ((0, 0), (0, LANES - experts)))
    router_three = jnp.stack(three_parts(router))

    weights = []
    first_in = expert_in.reshape(homes, local, depth, extent)
    second_in = expert_out.transpose(0, 2, 1).reshape(homes, local, depth, extent)
    for k in range(local):
        both = jnp.stack([first_in[:, k], second_in[:, k]], 1)
        mine = lax.all_to_all(both, ("i", "t"), 0, 0, tiled=True)
        if planes == 2:
            other = lax.ppermute(mine, "o", [(0, 1), (1, 0)])
            full = jnp.where(plane_at == 0, jnp.stack([mine, other]), jnp.stack([other, mine]))
        else:
            full = lax.all_gather(mine, "o", axis=0)
        weights.append(full.reshape(planes, inner, parts, 2, depth, extent))

    own_first = part_at * own_rows
    slot_index = jnp.where(slot_ids >= 0, expert_ids * CAP + slot_ids, -1)
    if parts == 2:
        slot_index = jnp.concatenate([
            lax.dynamic_slice_in_dim(slot_index, own_first, own_rows, 1),
            lax.dynamic_slice_in_dim(slot_index, own_rows - own_first, own_rows, 1)], 1)
    homes_i = lax.broadcasted_iota(jnp.int32, (inner, local, CAP), 0)
    locals_i = lax.broadcasted_iota(jnp.int32, (inner, local, CAP), 1)
    cap_i = lax.broadcasted_iota(jnp.int32, (inner, local, CAP), 2)
    places = ((homes_i * parts + part_at) * local + locals_i) * CAP + cap_i

    def table(m, positions, rows=slice(None)):
        index = slot_index[m, rows]
        flat = positions.reshape(1, -1)
        return ((index[:, 0:1] == flat) | (index[:, 1:2] == flat)).astype(low)

    def share(rows):
        if parts == 2:
            return jnp.concatenate([rows, lax.ppermute(rows, "t", [(0, 1), (1, 0)])], 1)
        return lax.all_gather(rows, "t", axis=1, tiled=True)

    def dispatch(shared):
        sent = []
        for m in range(micros):
            slots = mm(table(m, places), shared[m], TN).astype(low)
            slots = lax.all_to_all(slots.reshape(inner, local * CAP, width), "i", 0, 0, tiled=True)
            sent.append(slots.reshape(inner, local, CAP, width))
        return [
            jnp.concatenate([s[:, k].reshape(inner * CAP, width) for s in sent], 0) for k in range(local)]

    cot_slots = dispatch(share(cotangent.astype(low)))

    flags = lax.dynamic_slice_in_dim(key_mask, part_at * images, images, 1).reshape(total, 1, length)
    bias = jnp.where(flags > 0, 0.0, -1e30).astype(jnp.float32)
    tok = tokens.reshape(total, length, width)
    per_step = 2 if total % 2 == 0 else 1
    middle, routed, proj, mixed, gates = attention_forward(tok, bias, mats, norms, router, per_step)

    row_slots = dispatch(share(routed.reshape(micros, own_rows, width)))

    first_out, second_out, results, backs = [], [], [], []
    for k in range(local):
        expert = ((inner_at * parts + part_at) * local + k).astype(jnp.int32).reshape(1)
        result, back, dweights = run_expert(expert, row_slots[k], cot_slots[k], weights[k], router_three)
        results.append(result.reshape(micros, inner, CAP, width))
        backs.append(back.reshape(micros, inner, CAP, width + LANES))
        dweights = dweights.reshape(planes, homes, 2, depth, extent)
        if planes == 2:
            theirs = lax.dynamic_index_in_dim(dweights, 1 - plane_at, 0, keepdims=False)
            ours = lax.dynamic_index_in_dim(dweights, plane_at, 0, keepdims=False)
            summed = ours.astype(jnp.float32) + lax.ppermute(
                theirs, "o", [(0, 1), (1, 0)]).astype(jnp.float32)
            summed = summed.astype(low)
        else:
            summed = lax.psum_scatter(dweights, "o", scatter_dimension=0, tiled=True)[0]
        final = lax.all_to_all(summed, ("i", "t"), 0, 0, tiled=True)
        first_out.append(final[:, 0])
        second_out.append(final[:, 1])
    first_grad = jnp.stack(first_out, 1).reshape(experts, depth, extent).astype(jnp.float32)
    second_grad = jnp.stack(second_out, 1).reshape(experts, depth, extent).astype(jnp.float32)
    second_grad = second_grad.transpose(0, 2, 1)

    def collect(values):
        size = values[0].shape[-1]
        answers = []
        for m in range(micros):
            back = jnp.stack([v[m] for v in values], 1).reshape(inner, local * CAP, size)
            back = lax.all_to_all(back, "i", 0, 0, tiled=True).reshape(inner * local * CAP, size)
            if parts == 2:
                away = mm(table(m, places, slice(own_rows, None)), back).astype(low)
                here = mm(table(m, places, slice(0, own_rows)), back)
                answers.append(here + lax.ppermute(away, "t", [(0, 1), (1, 0)]).astype(jnp.float32))
            else:
                whole = mm(table(m, places), back).astype(low)
                answers.append(lax.psum_scatter(
                    whole, "t", scatter_dimension=0, tiled=True).astype(jnp.float32))
        return jnp.stack(answers)

    grad = collect(backs)
    combined = collect(results)
    block_out = middle.reshape(micros, own_rows, width) + combined

    input_grad, dmats, dnorms, drouter = attention_backward(
        tok, middle, cotangent.reshape(total, length, width), grad.reshape(total, length, width + LANES),
        gates, proj, mixed, bias, mats, norms, router.T, per_step)
    input_grad = input_grad.reshape(micros, own_rows, width)

    dmats = dmats.reshape(4, planes, inner, depth, parts, columns).transpose(2, 4, 1, 0, 3, 5)
    dmats = dmats.reshape(homes, planes, 4 * depth, columns)
    dloose = jnp.concatenate([dnorms.T, drouter[:, :experts]], 1)
    dloose = dloose.reshape(planes, inner, parts, small * (4 + experts)).transpose(1, 2, 0, 3)
    dloose = jnp.concatenate(three_parts(dloose), -1)
    dloose = jnp.pad(dloose, ((0, 0),) * 3 + ((0, loose_rows * columns - loose_count),))
    dloose = dloose.reshape(homes, planes, loose_rows, columns)
    payload = jnp.concatenate([dmats, dloose], 2)
    payload = lax.all_to_all(payload, ("i", "t"), 0, 0, tiled=True)
    payload = jnp.sum(payload.astype(jnp.float32), 0)
    if planes == 2:
        theirs = lax.dynamic_index_in_dim(payload, 1 - plane_at, 0, keepdims=False)
        ours = lax.dynamic_index_in_dim(payload, plane_at, 0, keepdims=False)
        reduced = ours + lax.ppermute(theirs, "o", [(0, 1), (1, 0)])
    else:
        reduced = lax.psum_scatter(payload, "o", scatter_dimension=0, tiled=True)[0]
    matrices = reduced[:4 * depth].reshape(4, depth, columns)
    qkv_grad = matrices[:3].transpose(1, 0, 2)
    out_grad = matrices[3].T
    tail = reduced[4 * depth:].reshape(-1)[:loose_count].reshape(3, small, 4 + experts)
    tail = (tail[0] + tail[1]) + tail[2]
    return (
        block_out, input_grad, tail[:, 0], tail[:, 1], qkv_grad, out_grad, tail[:, 2], tail[:, 3],
        tail[:, 4:], first_grad, second_grad,
    )


def solution(mesh):
    dp, parts = mesh.shape["dp"], mesh.shape["tensor"]
    inner = min(8, 32 // parts, dp)
    planes = dp // inner
    fine = Mesh(mesh.devices.reshape(planes, inner, parts), ("o", "i", "t"))
    dps = ("o", "i")
    every = ("o", "i", "t")
    rows = P(None, every, None)
    return jax.shard_map(
        functools.partial(per_device, planes, inner, parts),
        mesh=fine,
        in_specs=(
            rows, P(None, dps, None), P(None, dps, None), P(None, dps, None), P(every), P(every),
            P(dps, None, "t"), P("t", dps), P(every), P(every), P(every, None),
            P(None, dps, "t"), P(None, "t", dps), rows,
        ),
        out_specs=(
            rows, rows, P(every), P(every), P(dps, None, "t"), P("t", dps), P(every), P(every),
            P(every, None), P(None, dps, "t"), P(None, "t", dps),
        ),
        check_vma=False,
    )
```

time: 2160 us -> 1100 us (0.51)
  waiting for transfers between devices: 1100 us -> 672 us
  matrix products: 465 us -> 61.2 us
  local copies, waits for them, and re-layouts: 293 us -> 52.9 us
  blocking collectives: 186 us -> 0 us
  Pallas kernels: 0 us -> 159 us
  starting transfers between devices: 1.58 us -> 79.3 us
  other arithmetic: 82.1 us -> 55.2 us
    reduce_scatter x12 -> x0, waiting for transfers between devices: 812 us -> none  [the longest x1 330 us: per_device(): lax.psum_scatter(first_acc.astype(jnp.bfloat16), 'dp', scatter_dimension=...]
    ppermute x0 -> x11, waiting for transfers between devices: none -> 531 us  [the longest x2 176 us: per_device(): lax.ppermute(theirs, 'o', [(0, 1), (1, 0)]).astype(jnp.float32)]
    dot_general x48 -> x12, matrix products: 465 us -> 61.2 us  [mm(): lax.dot_general(a, b, dims, precision=precision, preferred_element_type=j...]
    all_gather x10 -> x2, waiting for transfers between devices: 286 us -> 30.1 us  [the longest x1 30 us: per_device(): gathered = lax.all_gather(gathered, 't', axis=0)]
    pallas_call x0 -> x4, Pallas kernels: none -> 159 us  [the longest x2 85.1 us: run_expert(): pl.pallas_call(expert_kernel, grid_spec=pltpu.PrefetchScalarGridSpec(num_...]
    gather x10 -> x0, local copies, waits for them, and re-layouts: 113 us -> none  [the longest x2 38.3 us: per_device(): gate_grads = gate_padded[slot_index]]
    all_to_all x0 -> x13, waiting for transfers between devices: none -> 111 us  [the longest x4 69.4 us: collect(): lax.all_to_all(back, 'i', 0, 0, tiled=True)]
    all_gather x3 -> x0, blocking collectives: 105 us -> none  [the longest x1 61.9 us: per_device(): lax.all_gather(router_weight, ('dp', 'tensor'), axis=0, tiled=True)]
  transfers between devices with their start and end apart: 25 -> 26, of which waited for: 11 -> 16; matrix products, arithmetic and copies ran while one was open for 35% -> 13% of each run, Pallas kernels for 0% -> 7%
where the time goes in v1:
time: 1100 us; the launch traced here: 1090 us
  waiting for transfers between devices  672 us (61%)
  Pallas kernels  159 us (14%)
  starting transfers between devices  79.3 us (7%)
  matrix products  61.2 us (6%)
  other arithmetic  55.2 us (5%)
  local copies, waits for them, and re-layouts  52.9 us (5%)
  between operations  14.9 us (1%)
    ppermute x2, waiting for transfers between devices, per_device(): lax.ppermute(theirs, 'o', [(0, 1), (1, 0)]).astype(jnp.float32)  176 us
    ppermute x2, waiting for transfers between devices, per_device(): other = lax.ppermute(mine, 'o', [(0, 1), (1, 0)])  168 us
    ppermute x2, waiting for transfers between devices, share(): return jnp.concatenate([rows, lax.ppermute(rows, 't', [(0, 1), (1, 0)])], 1)  92.9 us
    ppermute x4, waiting for transfers between devices, collect(): lax.ppermute(away, 't', [(0, 1), (1, 0)]).astype(jnp.float32)  89.4 us
    pallas_call x2, Pallas kernels, run_expert(): pl.pallas_call(expert_kernel, grid_spec=pltpu.PrefetchScalarGridSpec(num_...  85.1 us
    all_to_all x4, waiting for transfers between devices, collect(): lax.all_to_all(back, 'i', 0, 0, tiled=True)  69.4 us
    dot_general x12, matrix products, mm(): lax.dot_general(a, b, dims, precision=precision, preferred_element_type=j...  61.2 us
    pallas_call x1, Pallas kernels, attention_backward(): pl.pallas_call(backward_kernel, grid=(images // per_step,), in_specs=[row...  49.9 us
  transfers between devices with their start and end apart: 26, of which 16 were waited for; matrix products, arithmetic and copies ran while one was open for 13% of the time, Pallas kernels for 7%

profile of v1, /device:TPU:4, one launch (start us, length us, event | category | flops | bytes accessed | tf_op | source)
XLA Modules:
  0.0 1094.0 jit_solution(11109561719835333312)
XLA Ops:
  12.6 5.3 all-to-all-start.4
  20.6 24.2 %all-to-all-done.4 = bf16[16,2,32,1024]{3,2,1,0:T(8,128)(2,1)S(1)} async-done(((bf16[16,2,32,1024]{3,2,1,0:T(8,128)(2,1)}), bf16[16,2,32,1024]{3,2,1,0:T(8,128)(2,1)S(1)}, u32[]{:S(2)}, u32[]{:S(2)}) %all-to-all-start.4) | async-done | bytes 2097184 | tf_op jit(solution)/shard_map/all_to_all | solution.py:426
  44.8 5.3 all-to-all-start.5
  56.9 55.2 %collective-permute-done.1 = bf16[2,800,512]{2,1,0:T(8,128)(2,1)} collective-permute-done((bf16[2,800,512]{2,1,0:T(8,128)(2,1)}, bf16[2,800,512]{2,1,0:T(8,128)(2,1)}, u32[]{:S(2)}, u32[]{:S(2)}) %collective-permute-start.1) | collective-permute-done | bytes 1638432 | tf_op jit(solution)/shard_map/ppermute | solution.py:452
  112.1 7.2 fusion.53
  125.2 7.3 fusion.51
  132.4 30.0 %all-gather.7.cloned.1.call-done = bf16[32,144,256]{2,1,0:T(8,128)(2,1)} async-done(((bf16[16,144,256]{2,1,0:T(8,128)(2,1)}), bf16[32,144,256]{2,1,0:T(8,128)(2,1)}) %all-gather.7.cloned.1.call-update) | async-done | bytes 2359312 | tf_op jit(solution)/shard_map/all_gather | solution.py:409
  165.3 5.1 all-to-all-start.3
  180.7 23.7 %attention_forward.1 = (f32[8,200,512]{2,1,0:T(8,128)}, bf16[8,200,512]{2,1,0:T(8,128)(2,1)}, bf16[8,200,1536]{2,1,0:T(8,128)(2,1)}, bf16[8,200,512]{2,1,0:T(8,128)(2,1)}, f32[8,200,128]{2,1,0:T(8,128)}) custom-call(f32[8,200,512]{2,1,0:T(8,128)} %bitcast.237, f32[8,1,200]{2,1,0:T(1,128)} %select_n.47.bias_ref, bf16[4,512,512]{2,1,0:T(8,128)(2,1)} %reshape.288.mats_ref, ...), custom_call_target="tpu_custom_call" | custom-call | flops 4194304000 | bytes 13107200 | tf_op jit(solution)/shard_map/attention_forward/pallas_call | solution.py:119
  204.9 37.7 %collective-permute-done = bf16[2,800,512]{2,1,0:T(8,128)(2,1)S(1)} collective-permute-done((bf16[2,800,512]{2,1,0:T(8,128)(2,1)}, bf16[2,800,512]{2,1,0:T(8,128)(2,1)S(1)}, u32[]{:S(2)}, u32[]{:S(2)}) %collective-permute-start) | collective-permute-done | bytes 1638432 | tf_op jit(solution)/shard_map/ppermute | solution.py:452
  243.7 6.9 fusion.52
  255.4 6.9 fusion.50
  262.4 16.9 %all-to-all-done = bf16[8,240,512]{2,1,0:T(8,128)(2,1)} async-done(((bf16[8,240,512]{2,1,0:T(8,128)(2,1)}), bf16[8,240,512]{2,1,0:T(8,128)(2,1)}, u32[]{:S(2)}, u32[]{:S(2)}) %all-to-all-start) | async-done | bytes 1966112 | tf_op jit(solution)/shard_map/all_to_all | solution.py:459
  279.3 5.0 all-to-all-start.1
  295.1 128.7 %collective-permute-done.2 = bf16[16,2,32,1024]{3,2,1,0:T(8,128)(2,1)} collective-permute-done((bf16[16,2,32,1024]{3,2,1,0:T(8,128)(2,1)S(1)}, bf16[16,2,32,1024]{3,2,1,0:T(8,128)(2,1)}, u32[]{:S(2)}, u32[]{:S(2)}) %collective-permute-start.2) | collective-permute-done | bytes 2097184 | tf_op jit(solution)/shard_map/ppermute | solution.py:428
  428.3 39.6 %collective-permute-done.3 = bf16[16,2,32,1024]{3,2,1,0:T(8,128)(2,1)} collective-permute-done((bf16[16,2,32,1024]{3,2,1,0:T(8,128)(2,1)}, bf16[16,2,32,1024]{3,2,1,0:T(8,128)(2,1)}, u32[]{:S(2)}, u32[]{:S(2)}) %collective-permute-start.3) | collective-permute-done | bytes 2097184 | tf_op jit(solution)/shard_map/ppermute | solution.py:428
  467.9 6.0 maximum_select_fusion.1.weights_ref
  479.5 42.5 %expert.2 = (bf16[1920,512]{1,0:T(8,128)(2,1)}, bf16[1920,640]{1,0:T(8,128)(2,1)}, bf16[2,8,2,2,32,1024]{5,4,3,2,1,0:T(8,128)(2,1)}) custom-call(s32[1]{0:T(128)} %bitcast.18.expert_ref, bf16[1920,512]{1,0:T(8,128)(2,1)} %pad_maximum_fusion.8.slots_ref, bf16[1920,512]{1,0:T(8,128)(2,1)} %pad_maximum_fusion.9.cots_ref, ...), custom_call_target="tpu_custom_call" | custom-call | flops 24159191040 | bytes 16252928 | tf_op jit(solution)/shard_map/expert/pallas_call | solution.py:350
  525.3 42.6 %expert.3 = (bf16[1920,512]{1,0:T(8,128)(2,1)}, bf16[1920,640]{1,0:T(8,128)(2,1)}, bf16[2,8,2,2,32,1024]{5,4,3,2,1,0:T(8,128)(2,1)}) custom-call(s32[1]{0:T(128)} %bitcast.48.expert_ref, bf16[1920,512]{1,0:T(8,128)(2,1)} %pad_maximum_fusion.10.slots_ref, bf16[1920,512]{1,0:T(8,128)(2,1)} %pad_maximum_fusion.11.cots_ref, ...), custom_call_target="tpu_custom_call" | custom-call | flops 24159191040 | bytes 16252928 | tf_op jit(solution)/shard_map/expert/pallas_call | solution.py:350
  577.0 22.4 %all-to-all-done.6 = bf16[8,240,512]{2,1,0:T(8,128)(2,1)} async-done(((bf16[8,240,512]{2,1,0:T(8,128)(2,1)}), bf16[8,240,512]{2,1,0:T(8,128)(2,1)}, u32[]{:S(2)}, u32[]{:S(2)}) %all-to-all-start.6) | async-done | bytes 1966112 | tf_op jit(solution)/shard_map/all_to_all | solution.py:501
  608.5 19.5 %all-to-all-done.7 = bf16[8,240,512]{2,1,0:T(8,128)(2,1)} async-done(((bf16[8,240,512]{2,1,0:T(8,128)(2,1)}), bf16[8,240,512]{2,1,0:T(8,128)(2,1)}, u32[]{:S(2)}, u32[]{:S(2)}) %all-to-all-start.7) | async-done | bytes 1966112 | tf_op jit(solution)/shard_map/all_to_all | solution.py:501
  628.1 4.8 all-to-all-start.8
  634.6 27.5 %all-to-all-done.8 = bf16[8,240,640]{2,1,0:T(8,128)(2,1)} async-done(((bf16[8,240,640]{2,1,0:T(8,128)(2,1)}), bf16[8,240,640]{2,1,0:T(8,128)(2,1)}, u32[]{:S(2)}, u32[]{:S(2)}) %all-to-all-start.8) | async-done | bytes 2457632 | tf_op jit(solution)/shard_map/all_to_all | solution.py:501
  671.6 91.9 %collective-permute-done.9 = bf16[16,2,32,1024]{3,2,1,0:T(8,128)(2,1)} collective-permute-done((bf16[16,2,32,1024]{3,2,1,0:T(8,128)(2,1)}, bf16[16,2,32,1024]{3,2,1,0:T(8,128)(2,1)}, u32[]{:S(2)}, u32[]{:S(2)}) %collective-permute-start.9) | collective-permute-done | bytes 2097184 | tf_op jit(solution)/shard_map/ppermute | solution.py:484
  779.1 5.7 fusion.67
  786.3 84.2 %collective-permute-done.10 = bf16[16,2,32,1024]{3,2,1,0:T(8,128)(2,1)} collective-permute-done((bf16[16,2,32,1024]{3,2,1,0:T(8,128)(2,1)}, bf16[16,2,32,1024]{3,2,1,0:T(8,128)(2,1)}, u32[]{:S(2)}, u32[]{:S(2)}) %collective-permute-start.10) | collective-permute-done | bytes 2097184 | tf_op jit(solution)/shard_map/ppermute | solution.py:484
  875.7 5.1 all-to-all-start.12
  887.0 5.0 add_bitcast_fusion.1
  891.9 37.6 %collective-permute-done.7 = bf16[800,640]{1,0:T(8,128)(2,1)S(1)} collective-permute-done((bf16[800,640]{1,0:T(8,128)(2,1)S(1)}, bf16[800,640]{1,0:T(8,128)(2,1)S(1)}, u32[]{:S(2)}, u32[]{:S(2)}) %collective-permute-start.7) | collective-permute-done | bytes 1024032 | tf_op jit(solution)/shard_map/ppermute | solution.py:505
  934.7 49.9 %attention_backward.1 = (f32[8,200,512]{2,1,0:T(8,128)}, bf16[4,512,512]{2,1,0:T(8,128)(2,1)}, f32[4,512]{1,0:T(4,128)}, f32[512,128]{1,0:T(8,128)}) custom-call(f32[8,200,512]{2,1,0:T(8,128)} %bitcast.238, f32[8,200,512]{2,1,0:T(8,128)} %get-tuple-element.26.middle_ref, f32[8,200,512]{2,1,0:T(8,128)} %bitcast.212, f32[8,200,640]{2,1,0:T(8,128)} %bitcast.199, ...), custom_call_target="tpu_custom_call" | custom-call | flops 12582912000 | bytes 24576000 | tf_op jit(solution)/shard_map/attention_backward/pallas_call | solution.py:235
  1006.4 38.2 %collective-permute-done.4 = bf16[800,512]{1,0:T(8,128)(2,1)S(1)} collective-permute-done((bf16[800,512]{1,0:T(8,128)(2,1)S(1)}, bf16[800,512]{1,0:T(8,128)(2,1)S(1)}, u32[]{:S(2)}, u32[]{:S(2)}) %collective-permute-start.4) | collective-permute-done | bytes 819232 | tf_op jit(solution)/shard_map/ppermute | solution.py:505
  1048.0 13.5 %collective-permute-done.5 = bf16[800,512]{1,0:T(8,128)(2,1)S(1)} collective-permute-done((bf16[800,512]{1,0:T(8,128)(2,1)S(1)}, bf16[800,512]{1,0:T(8,128)(2,1)S(1)}, u32[]{:S(2)}, u32[]{:S(2)}) %collective-permute-start.5) | collective-permute-done | bytes 819232 | tf_op jit(solution)/shard_map/ppermute | solution.py:505
  (181 shorter events, 177.7 us)
Async XLA Ops:
  12.6 32.2 %all-to-all-start.4 = ((bf16[16,2,32,1024]{3,2,1,0:T(8,128)(2,1)}), bf16[16,2,32,1024]{3,2,1,0:T(8,128)(2,1)S(1)}, u32[]{:S(2)}, u32[]{:S(2)}) async-start(bf16[16,2,32,1024]{3,2,1,0:T(8,128)(2,1)} %pad_maximum_fusion.4), calls=%async_computation.4 | async-start | bytes 4194304 | tf_op jit(solution)/shard_map/all_to_all | solution.py:426
  44.8 8.8 copy-start.3
  44.8 74.5 %all-to-all-start.5 = ((bf16[16,2,32,1024]{3,2,1,0:T(8,128)(2,1)}), bf16[16,2,32,1024]{3,2,1,0:T(8,128)(2,1)}, u32[]{:S(2)}, u32[]{:S(2)}) async-start(bf16[16,2,32,1024]{3,2,1,0:T(8,128)(2,1)} %pad_maximum_fusion.5), calls=%async_computation.5 | async-start | bytes 4194304 | tf_op jit(solution)/shard_map/all_to_all | solution.py:426
  50.2 6.4 copy-start.12
  50.2 6.4 copy-start.13
  50.2 73.8 %all-gather.5.cloned.1.call-start = ((), (), s32[]{:S(2)}) async-start(), calls=%async_computation.13 | async-start | bytes 1253376 | tf_op jit(solution)/shard_map/all_gather | solution.py:408
  53.6 58.5 %collective-permute-start.1 = (bf16[2,800,512]{2,1,0:T(8,128)(2,1)}, bf16[2,800,512]{2,1,0:T(8,128)(2,1)}, u32[]{:S(2)}, u32[]{:S(2)}) collective-permute-start(bf16[2,800,512]{2,1,0:T(8,128)(2,1)} %convert_element_type.156), channel_id=1, source_target_pairs={{0,1},{1,0},{2,3},{3,2},{4,5},{5,4},{6,7},{7,6},{8,9},{9,8},{10,11... | collective-permute-start | bytes 4915208 | tf_op jit(solution)/shard_map/ppermute | solution.py:452
  119.3 46.0 %all-to-all-start.2 = ((bf16[8,240,512]{2,1,0:T(8,128)(2,1)}), bf16[8,240,512]{2,1,0:T(8,128)(2,1)}, u32[]{:S(2)}, u32[]{:S(2)}) async-start(bf16[8,240,512]{2,1,0:T(8,128)(2,1)} %bitcast.31), calls=%async_computation.2 | async-start | bytes 3932160 | tf_op jit(solution)/shard_map/all_to_all | solution.py:459
  123.8 38.7 %all-gather.7.cloned.1.call-start = ((), (), s32[]{:S(2)}) async-start(), calls=%async_computation.14 | async-start | bytes 3538944 | tf_op jit(solution)/shard_map/all_gather | solution.py:409
  165.3 85.4 %all-to-all-start.3 = ((bf16[8,240,512]{2,1,0:T(8,128)(2,1)}), bf16[8,240,512]{2,1,0:T(8,128)(2,1)}, u32[]{:S(2)}, u32[]{:S(2)}) async-start(bf16[8,240,512]{2,1,0:T(8,128)(2,1)} %bitcast.223), calls=%async_computation.3 | async-start | bytes 3932160 | tf_op jit(solution)/shard_map/all_to_all | solution.py:459
  204.5 38.1 %collective-permute-start = (bf16[2,800,512]{2,1,0:T(8,128)(2,1)}, bf16[2,800,512]{2,1,0:T(8,128)(2,1)S(1)}, u32[]{:S(2)}, u32[]{:S(2)}) collective-permute-start(bf16[2,800,512]{2,1,0:T(8,128)(2,1)} %bitcast.239), channel_id=1, source_target_pairs={{0,1},{1,0},{2,3},{3,2},{4,5},{5,4},{6,7},{7,6},{8,9},{9,8},{10,11... | collective-permute-start | bytes 4915208 | tf_op jit(solution)/shard_map/ppermute | solution.py:452
  250.7 28.6 %all-to-all-start = ((bf16[8,240,512]{2,1,0:T(8,128)(2,1)}), bf16[8,240,512]{2,1,0:T(8,128)(2,1)}, u32[]{:S(2)}, u32[]{:S(2)}) async-start(bf16[8,240,512]{2,1,0:T(8,128)(2,1)} %bitcast.22), calls=%async_computation | async-start | bytes 3932160 | tf_op jit(solution)/shard_map/all_to_all | solution.py:459
  262.4 22.0 %copy-start.4 = (bf16[16,2,32,1024]{3,2,1,0:T(8,128)(2,1)S(1)}, bf16[16,2,32,1024]{3,2,1,0:T(8,128)(2,1)}, u32[]{:S(2)}) copy-start(bf16[16,2,32,1024]{3,2,1,0:T(8,128)(2,1)} %copy-done.3) | copy-start | bytes 6291460
  279.3 196.2 %all-to-all-start.1 = ((bf16[8,240,512]{2,1,0:T(8,128)(2,1)}), bf16[8,240,512]{2,1,0:T(8,128)(2,1)}, u32[]{:S(2)}, u32[]{:S(2)}) async-start(bf16[8,240,512]{2,1,0:T(8,128)(2,1)} %bitcast.222), calls=%async_computation.1 | async-start | bytes 3932160 | tf_op jit(solution)/shard_map/all_to_all | solution.py:459
  284.3 139.5 %collective-permute-start.2 = (bf16[16,2,32,1024]{3,2,1,0:T(8,128)(2,1)S(1)}, bf16[16,2,32,1024]{3,2,1,0:T(8,128)(2,1)}, u32[]{:S(2)}, u32[]{:S(2)}) collective-permute-start(bf16[16,2,32,1024]{3,2,1,0:T(8,128)(2,1)S(1)} %copy-done.4), channel_id=1, source_target_pairs={{0,16},{16,0},{1,17},{17,1},{2,18},{18,2},{3,19},{19,3},{4,20},{20... | collective-permute-start | bytes 6291464 | tf_op jit(solution)/shard_map/ppermute | solution.py:428
  286.8 181.1 %collective-permute-start.3 = (bf16[16,2,32,1024]{3,2,1,0:T(8,128)(2,1)}, bf16[16,2,32,1024]{3,2,1,0:T(8,128)(2,1)}, u32[]{:S(2)}, u32[]{:S(2)}) collective-permute-start(bf16[16,2,32,1024]{3,2,1,0:T(8,128)(2,1)} %all-to-all-done.5), channel_id=1, source_target_pairs={{0,16},{16,0},{1,17},{17,1},{2,18},{18,2},{3,19},{19,3},{4,20},{20... | collective-permute-start | bytes 6291464 | tf_op jit(solution)/shard_map/ppermute | solution.py:428
  570.9 28.5 %all-to-all-start.6 = ((bf16[8,240,512]{2,1,0:T(8,128)(2,1)}), bf16[8,240,512]{2,1,0:T(8,128)(2,1)}, u32[]{:S(2)}, u32[]{:S(2)}) async-start(bf16[8,240,512]{2,1,0:T(8,128)(2,1)} %bitcast.58), calls=%async_computation.6 | async-start | bytes 3932160 | tf_op jit(solution)/shard_map/all_to_all | solution.py:501
  599.4 28.6 %all-to-all-start.7 = ((bf16[8,240,512]{2,1,0:T(8,128)(2,1)}), bf16[8,240,512]{2,1,0:T(8,128)(2,1)}, u32[]{:S(2)}, u32[]{:S(2)}) async-start(bf16[8,240,512]{2,1,0:T(8,128)(2,1)} %bitcast.67), calls=%async_computation.7 | async-start | bytes 3932160 | tf_op jit(solution)/shard_map/all_to_all | solution.py:501
  628.1 34.0 %all-to-all-start.8 = ((bf16[8,240,640]{2,1,0:T(8,128)(2,1)}), bf16[8,240,640]{2,1,0:T(8,128)(2,1)}, u32[]{:S(2)}, u32[]{:S(2)}) async-start(bf16[8,240,640]{2,1,0:T(8,128)(2,1)} %bitcast.76), calls=%async_computation.8 | async-start | bytes 4915200 | tf_op jit(solution)/shard_map/all_to_all | solution.py:501
  662.0 106.0 %all-to-all-start.9 = ((bf16[8,240,640]{2,1,0:T(8,128)(2,1)}), bf16[8,240,640]{2,1,0:T(8,128)(2,1)S(1)}, u32[]{:S(2)}, u32[]{:S(2)}) async-start(bf16[8,240,640]{2,1,0:T(8,128)(2,1)} %bitcast.83), calls=%async_computation.9 | async-start | bytes 4915200 | tf_op jit(solution)/shard_map/all_to_all | solution.py:501
  669.6 93.9 %collective-permute-start.9 = (bf16[16,2,32,1024]{3,2,1,0:T(8,128)(2,1)}, bf16[16,2,32,1024]{3,2,1,0:T(8,128)(2,1)}, u32[]{:S(2)}, u32[]{:S(2)}) collective-permute-start(bf16[16,2,32,1024]{3,2,1,0:T(8,128)(2,1)} %dynamic-slice_bitcast_fusion.1), channel_id=1, source_target_pairs={{0,16},{16,0},{1,17},{17,1},{2,18},{18,2},{3,19},{19,3},{4,20},{20... | collective-permute-start | bytes 6291464 | tf_op jit(solution)/shard_map/ppermute | solution.py:484
  769.5 104.9 %all-to-all-start.11 = ((bf16[16,2,32,1024]{3,2,1,0:T(8,128)(2,1)}), bf16[16,2,32,1024]{3,2,1,0:T(8,128)(2,1)S(1)}, u32[]{:S(2)}, u32[]{:S(2)}) async-start(bf16[16,2,32,1024]{3,2,1,0:T(8,128)(2,1)} %fusion.25), calls=%async_computation.11 | async-start | bytes 4194304 | tf_op jit(solution)/shard_map/all_to_all | solution.py:489
  776.6 93.9 %collective-permute-start.10 = (bf16[16,2,32,1024]{3,2,1,0:T(8,128)(2,1)}, bf16[16,2,32,1024]{3,2,1,0:T(8,128)(2,1)}, u32[]{:S(2)}, u32[]{:S(2)}) collective-permute-start(bf16[16,2,32,1024]{3,2,1,0:T(8,128)(2,1)} %dynamic-slice_bitcast_fusion), channel_id=1, source_target_pairs={{0,16},{16,0},{1,17},{17,1},{2,18},{18,2},{3,19},{19,3},{4,20},{20... | collective-permute-start | bytes 6291464 | tf_op jit(solution)/shard_map/ppermute | solution.py:484
  779.1 91.3 %copy-start.5 = (bf16[2,8,2,2,32,1024]{5,4,3,2,1,0:T(8,128)(2,1)S(1)}, bf16[2,8,2,2,32,1024]{5,4,3,2,1,0:T(8,128)(2,1)}, u32[]{:S(2)}) copy-start(bf16[2,8,2,2,32,1024]{5,4,3,2,1,0:T(8,128)(2,1)} %get-tuple-element.40) | copy-start | bytes 12582916
  784.8 102.1 %collective-permute-start.6 = (bf16[800,640]{1,0:T(8,128)(2,1)}, bf16[800,640]{1,0:T(8,128)(2,1)}, u32[]{:S(2)}, u32[]{:S(2)}) collective-permute-start(bf16[800,640]{1,0:T(8,128)(2,1)} %fusion.67), channel_id=1, source_target_pairs={{0,1},{1,0},{2,3},{3,2},{4,5},{5,4},{6,7},{7,6},{8,9},{9,8},{10,11... | collective-permute-start | bytes 3072008 | tf_op jit(solution)/shard_map/ppermute | solution.py:505
  875.7 116.5 %all-to-all-start.12 = ((bf16[16,2,32,1024]{3,2,1,0:T(8,128)(2,1)}), bf16[16,2,32,1024]{3,2,1,0:T(8,128)(2,1)}, u32[]{:S(2)}, u32[]{:S(2)}) async-start(bf16[16,2,32,1024]{3,2,1,0:T(8,128)(2,1)} %fusion.24), calls=%async_computation.12 | async-start | bytes 4194304 | tf_op jit(solution)/shard_map/all_to_all | solution.py:489
  885.4 44.2 %collective-permute-start.7 = (bf16[800,640]{1,0:T(8,128)(2,1)S(1)}, bf16[800,640]{1,0:T(8,128)(2,1)S(1)}, u32[]{:S(2)}, u32[]{:S(2)}) collective-permute-start(bf16[800,640]{1,0:T(8,128)(2,1)S(1)} %fusion.66), channel_id=1, source_target_pairs={{0,1},{1,0},{2,3},{3,2},{4,5},{5,4},{6,7},{7,6},{8,9},{9,8},{10,11... | collective-permute-start | bytes 3072008 | tf_op jit(solution)/shard_map/ppermute | solution.py:505
  887.0 42.6 %copy-start.9 = (bf16[8,240,640]{2,1,0:T(8,128)(2,1)S(1)}, bf16[8,240,640]{2,1,0:T(8,128)(2,1)}, u32[]{:S(2)}) copy-start(bf16[8,240,640]{2,1,0:T(8,128)(2,1)} %copy-done.8) | copy-start | bytes 7372804
  992.2 81.9 %all-to-all-start.10 = ((bf16[16,2,144,256]{3,2,1,0:T(8,128)(2,1)}), bf16[16,2,144,256]{3,2,1,0:T(8,128)(2,1)S(1)}, u32[]{:S(2)}, u32[]{:S(2)}) async-start(bf16[16,2,144,256]{3,2,1,0:T(8,128)(2,1)} %pad_maximum_fusion.3), calls=%async_computation.10 | async-start | bytes 4718592 | tf_op jit(solution)/shard_map/all_to_all | solution.py:529
  1000.4 44.2 %collective-permute-start.4 = (bf16[800,512]{1,0:T(8,128)(2,1)S(1)}, bf16[800,512]{1,0:T(8,128)(2,1)S(1)}, u32[]{:S(2)}, u32[]{:S(2)}) collective-permute-start(bf16[800,512]{1,0:T(8,128)(2,1)S(1)} %fusion.69), channel_id=1, source_target_pairs={{0,1},{1,0},{2,3},{3,2},{4,5},{5,4},{6,7},{7,6},{8,9},{9,8},{10,11... | collective-permute-start | bytes 2457608 | tf_op jit(solution)/shard_map/ppermute | solution.py:505
  1005.8 55.8 %collective-permute-start.5 = (bf16[800,512]{1,0:T(8,128)(2,1)S(1)}, bf16[800,512]{1,0:T(8,128)(2,1)S(1)}, u32[]{:S(2)}, u32[]{:S(2)}) collective-permute-start(bf16[800,512]{1,0:T(8,128)(2,1)S(1)} %fusion.68), channel_id=1, source_target_pairs={{0,1},{1,0},{2,3},{3,2},{4,5},{5,4},{6,7},{7,6},{8,9},{9,8},{10,11... | collective-permute-start | bytes 2457608 | tf_op jit(solution)/shard_map/ppermute | solution.py:505
  1074.5 9.6 collective-permute-start.8
  (17 other events, 63.9 us)
Sparse Core Ops, SparseCore 0:
  56.5 40.9 all-gather.4
  126.1 36.2 all-gather.6

commit v2 on v1

--- a/solution.py
+++ b/solution.py
@@ -52,31 +52,42 @@
     return lax.broadcasted_iota(jnp.int32, shape, 1) < HEAD
 
 
-def forward_kernel(
-    tok_ref, bias_ref, mats_ref, norms_ref, router_ref,
-    middle_ref, routed_ref, proj_ref, mixed_ref, gates_ref,
-):
-    images, length, width = tok_ref.shape
+def router_gates(routed, parts):
+    logits = mm(routed, parts, NT)
+    logits = logits + pltpu.roll(logits, LANES - 32, 1) + pltpu.roll(logits, LANES - 64, 1)
+    lane = lax.broadcasted_iota(jnp.int32, logits.shape, 1)
+    logits = jnp.where(lane < 32, logits, -1e30)
+    lifted = jnp.exp(logits - jnp.max(logits, -1, keepdims=True))
+    return lifted / jnp.sum(lifted, -1, keepdims=True)
+
+
+def forward_rows(first, images, tok_ref, bias_ref, mats_ref, norms_ref, parts_ref,
+                 middle_ref, proj_ref, mixed_ref, gates_ref):
+    _, length, width = tok_ref.shape
+    pieces, _, _, columns = mats_ref.shape
     rows = images * length
-    tok = tok_ref[...].reshape(rows, width)
+    here = pl.ds(first, images)
+    tok = tok_ref[here].reshape(rows, width)
     unit, _ = standardize(tok)
     normed = (unit * norms_ref[0:1] + norms_ref[1:2]).astype(jnp.bfloat16)
     for c in range(3):
-        part = mm(normed, mats_ref[c]).reshape(images, length, width)
-        for b in range(images):
-            proj_ref[b, :, c * width:(c + 1) * width] = part[b].astype(jnp.bfloat16)
+        for p in range(pieces):
+            part = mm(normed, mats_ref[p, c]).reshape(images, length, columns)
+            base = c * width + p * columns
+            for b in range(images):
+                proj_ref[first + b, :, base:base + columns] = part[b].astype(jnp.bfloat16)
     even = even_lanes((length, LANES))
     scale = jnp.bfloat16(HEAD ** -0.5)
     zero = jnp.zeros((), jnp.bfloat16)
     attended = []
     for b in range(images):
-        bias = bias_ref[b]
-        pieces = []
+        bias = bias_ref[first + b]
+        parts = []
         for pair in range(width // LANES):
             lanes = slice(pair * LANES, (pair + 1) * LANES)
-            query = proj_ref[b, :, lanes] * scale
-            keyed = proj_ref[b, :, width + pair * LANES:width + (pair + 1) * LANES]
-            valued = proj_ref[b, :, 2 * width + pair * LANES:2 * width + (pair + 1) * LANES]
+            query = proj_ref[first + b, :, lanes] * scale
+            keyed = proj_ref[first + b, :, width + pair * LANES:width + (pair + 1) * LANES]
+            valued = proj_ref[first + b, :, 2 * width + pair * LANES:2 * width + (pair + 1) * LANES]
             halves = []
             for odd in range(2):
                 chosen = jnp.where(even != bool(odd), query, zero)
@@ -85,22 +96,29 @@
                 probs = lifted * (1.0 / jnp.sum(lifted, -1, keepdims=True))
                 halves.append(mm(probs.astype(jnp.bfloat16), valued))
             both = jnp.where(even, halves[0], halves[1])
-            mixed_ref[b, :, lanes] = both.astype(jnp.bfloat16)
-            pieces.append(both)
-        attended.append(jnp.concatenate(pieces, 1))
+            mixed_ref[first + b, :, lanes] = both.astype(jnp.bfloat16)
+            parts.append(both)
+        attended.append(jnp.concatenate(parts, 1))
     joined = jnp.concatenate(attended, 0).astype(jnp.bfloat16)
-    middle = tok + mm(joined, mats_ref[3], NT)
-    middle_ref[...] = middle.reshape(images, length, width)
+    middle = tok
+    for p in range(pieces):
+        middle += mm(joined[:, p * columns:(p + 1) * columns], mats_ref[p, 3], NT)
+    middle_ref[here] = middle.reshape(images, length, width)
     unit, _ = standardize(middle)
-    routed = (unit * norms_ref[2:3] + norms_ref[3:4]).astype(jnp.bfloat16)
-    wide = routed.astype(jnp.float32)
-    routed_ref[...] = wide.reshape(images, length, width).astype(jnp.bfloat16)
-    logits = mm(wide, router_ref[...], NN, HIGH)
-    lane = lax.broadcasted_iota(jnp.int32, logits.shape, 1)
-    logits = jnp.where(lane < 32, logits, -1e30)
-    lifted = jnp.exp(logits - jnp.max(logits, -1, keepdims=True))
-    gates = lifted / jnp.sum(lifted, -1, keepdims=True)
-    gates_ref[...] = gates.reshape(images, length, LANES)
+    routed = unit * norms_ref[2:3] + norms_ref[3:4]
+    low = routed.astype(jnp.bfloat16)
+    gates_ref[here] = router_gates(low, parts_ref[...]).reshape(images, length, LANES)
+    return routed, low
+
+
+def forward_kernel(
+    tok_ref, bias_ref, mats_ref, norms_ref, parts_ref,
+    middle_ref, routed_ref, proj_ref, mixed_ref, gates_ref,
+):
+    images, length, width = tok_ref.shape
+    routed, _ = forward_rows(0, images, tok_ref, bias_ref, mats_ref, norms_ref, parts_ref,
+                             middle_ref, proj_ref, mixed_ref, gates_ref)
+    routed_ref[...] = routed.reshape(images, length, width).astype(jnp.bfloat16)
 
 
 def attention_forward(tok, bias, mats, norms, router, per_step):
@@ -166,8 +184,13 @@
     middle_grad = flat(cot_ref) + norm_back(routed_grad * norms_ref[2:3], unit, inverse)
     attn_cot = middle_grad.astype(jnp.bfloat16)
     joined = jnp.concatenate([mixed_ref[b].astype(jnp.float32) for b in range(images)], 0)
-    dmats_acc[3] += mm(attn_cot, joined.astype(jnp.bfloat16), TN)
-    mixed_grad = mm(attn_cot, mats_ref[3]).reshape(images, length, width)
+    joined = joined.astype(jnp.bfloat16)
+    pieces, _, _, columns = mats_ref.shape
+    spans = [slice(p * columns, (p + 1) * columns) for p in range(pieces)]
+    for p in range(pieces):
+        dmats_acc[p, 3] += mm(attn_cot, joined[:, spans[p]], TN)
+    mixed_grad = jnp.concatenate([mm(attn_cot, mats_ref[p, 3]) for p in range(pieces)], 1)
+    mixed_grad = mixed_grad.reshape(images, length, width)
     even = even_lanes((length, LANES))
     zero = jnp.zeros((), jnp.bfloat16)
     scale = jnp.bfloat16(HEAD ** -0.5)
@@ -211,8 +234,9 @@
     normed_grad = jnp.zeros((rows, width), jnp.float32)
     for c in range(3):
         part = dproj_ref[:, c * width:(c + 1) * width].astype(jnp.bfloat16)
-        dmats_acc[c] += mm(normed, part, TN)
-        normed_grad += mm(part, mats_ref[c], NT)
+        for p in range(pieces):
+            dmats_acc[p, c] += mm(normed, part[:, spans[p]], TN)
+            normed_grad += mm(part[:, spans[p]], mats_ref[p, c], NT)
     dnorms_ref[0:1] += jnp.sum(normed_grad * unit, 0, keepdims=True)
     dnorms_ref[1:2] += jnp.sum(normed_grad, 0, keepdims=True)
     input_grad = middle_grad + norm_back(normed_grad * norms_ref[0:1], unit, inverse)
@@ -278,13 +302,10 @@
         def prepare(r, carry):
             here = pl.ds(pl.multiple_of(r * chunk, 16), chunk)
             slots = slots_ref[here]
-            logits = mm(slots, router_ref[0]) + mm(slots, router_ref[1]) + mm(slots, router_ref[2])
-            lane = lax.broadcasted_iota(jnp.int32, logits.shape, 1)
-            logits = jnp.where(lane < 32, logits, -1e30)
-            lifted = jnp.exp(logits - jnp.max(logits, -1, keepdims=True))
-            gates = lifted / jnp.sum(lifted, -1, keepdims=True)
+            gates = router_gates(slots, router_ref[...])
+            lane = lax.broadcasted_iota(jnp.int32, gates.shape, 1)
             gate = jnp.sum(jnp.where(lane == expert_ref[0], gates, 0.0), -1, keepdims=True)
-            gate_scr[here] = jnp.broadcast_to(gate, logits.shape)
+            gate_scr[here] = jnp.broadcast_to(gate, gates.shape)
             low = (cots_ref[here].astype(jnp.float32) * gate).astype(jnp.bfloat16)
             grads[here] = low
             rows_t[r] = slots.T
@@ -379,6 +400,237 @@
     )(expert, slots, cots, weights, router)
 
 
+def flipped(position, bit):
+    return position + bit - 2 * bit * lax.rem(position // bit, 2)
+
+
+def to_peer(source, target, sends, receives, where):
+    return pltpu.make_async_remote_copy(
+        src_ref=source, dst_ref=target, send_sem=sends, recv_sem=receives, device_id=where,
+        device_id_type=pl.DeviceIdType.MESH)
+
+
+class Dispatch:
+    def __init__(self, index_ref, shared, staged, out, sends, receives, keep, inner, parts, local):
+        self.index_ref, self.shared, self.staged, self.out = index_ref, shared, staged, out
+        self.sends, self.receives, self.keep = sends, receives, keep
+        self.inner, self.parts, self.local = inner, parts, local
+        self.at_i, self.at_t = lax.axis_index("i"), lax.axis_index("t")
+
+    def copy(self, m, d, k):
+        home = lax.rem(self.at_i + d, self.inner)
+        target = self.out.at[k, pl.ds(pl.multiple_of((m * self.inner + self.at_i) * CAP, 8), CAP)]
+        return to_peer(self.staged.at[m, d, k], target, self.sends.at[m, d, k],
+                       self.receives.at[m, d, k], {"i": home})
+
+    def kept(self, m, k):
+        target = self.out.at[k, pl.ds(pl.multiple_of((m * self.inner + self.at_i) * CAP, 8), CAP)]
+        return pltpu.make_async_copy(self.staged.at[m, 0, k], target, self.keep.at[m, k])
+
+    def fill(self, m, d):
+        home = lax.rem(self.at_i + d, self.inner)
+        count = self.local * CAP
+        base = (home * self.parts + self.at_t) * count
+        places = base + lax.broadcasted_iota(jnp.int32, (count, 1), 0)
+        total = None
+        for half in range(2):
+            first = self.index_ref[m, 0, half:half + 1]
+            second = self.index_ref[m, 1, half:half + 1]
+            hits = jnp.where((first == places) | (second == places), 1.0, 0.0).astype(jnp.bfloat16)
+            part = mm(hits, self.shared[m, half])
+            total = part if total is None else total + part
+        for k in range(self.local):
+            self.staged[m, d, k] = total[k * CAP:(k + 1) * CAP].astype(jnp.bfloat16)
+
+    def send(self, m):
+        def step(d, carry):
+            self.fill(m, d)
+            for k in range(self.local):
+                self.copy(m, d, k).start()
+            return carry
+
+        lax.fori_loop(1, self.inner, step, 0)
+        self.fill(m, 0)
+        for k in range(self.local):
+            self.kept(m, k).start()
+
+    def finish(self, m):
+        def step(d, carry):
+            for k in range(self.local):
+                self.copy(m, d, k).wait()
+            return carry
+
+        lax.fori_loop(1, self.inner, step, 0)
+        for k in range(self.local):
+            self.kept(m, k).wait()
+
+
+def spread_kernel(
+    local, pack_ref, cot_ref, index_ref,
+    mats_ref, norms_ref, parts_ref, router_ref, cots_ref,
+    gathered, loose, shared, staged,
+    load, ring_send, ring_recv, pair_send, pair_recv, slot_send, slot_recv, slot_keep,
+):
+    at_o, at_i, at_t = (lax.axis_index(name) for name in ("o", "i", "t"))
+    micros = cot_ref.shape[0]
+    pieces, kinds, width, columns = mats_ref.shape
+    depth = width // 16
+    fill = pltpu.make_async_copy(pack_ref, gathered.at[0], load)
+    fill.start()
+    stages = [
+        {"t": 1 - at_t}, {"o": 1 - at_o}, {"i": flipped(at_i, 4)}, {"i": flipped(at_i, 2)},
+        {"i": flipped(at_i, 1)},
+    ]
+
+    def stage(j):
+        size = 2 ** j
+        return to_peer(gathered.at[pl.ds(0, size)], gathered.at[pl.ds(size, size)],
+                       ring_send.at[j], ring_recv.at[j], stages[j])
+
+    def swap(m):
+        return to_peer(shared.at[m, 0], shared.at[m, 1], pair_send.at[m], pair_recv.at[m],
+                       {"t": 1 - at_t})
+
+    plan = Dispatch(index_ref, shared, staged, cots_ref, slot_send, slot_recv, slot_keep, 8, 2, local)
+    fill.wait()
+    stage(0).start()
+    for m in range(micros):
+        shared[m, 0] = cot_ref[m].astype(jnp.bfloat16)
+    stage(0).wait()
+    stage(1).start()
+    for m in range(micros):
+        swap(m).start()
+    stage(1).wait()
+    stage(2).start()
+    stage(2).wait()
+    stage(3).start()
+    stage(3).wait()
+    stage(4).start()
+    swap(0).wait()
+    plan.send(0)
+    stage(4).wait()
+
+    def place(r, carry):
+        o = flipped_if(at_o, 1, lax.rem(r // 2, 2))
+        i = flipped_if(at_i, 4, lax.rem(r // 4, 2))
+        i = flipped_if(i, 2, lax.rem(r // 8, 2))
+        i = flipped_if(i, 1, lax.rem(r // 16, 2))
+        t = flipped_if(at_t, 1, lax.rem(r, 2))
+        row = pl.multiple_of((o * 8 + i) * depth, depth)
+        for c in range(kinds):
+            mats_ref[t, c, pl.ds(row, depth)] = gathered[r, c * depth:(c + 1) * depth]
+        loose[(o * 8 + i) * 2 + t] = gathered[r, kinds * depth:, 0:LANES].astype(jnp.float32)
+        return carry
+
+    lax.fori_loop(0, gathered.shape[0], place, 0)
+    turned = loose[...].reshape(width, LANES).T
+    norms_ref[...] = turned[96:104] + turned[104:112] + turned[112:120]
+    low = turned[0:96].astype(jnp.bfloat16)
+    parts_ref[...] = jnp.concatenate([low, jnp.zeros((32, width), jnp.bfloat16)], 0)
+    router_ref[0:32] = turned[0:32] + turned[32:64] + turned[64:96]
+    router_ref[32:] = jnp.zeros((96, width), jnp.float32)
+    for m in range(1, micros):
+        swap(m).wait()
+        plan.send(m)
+    for m in range(micros):
+        plan.finish(m)
+
+
+def flipped_if(position, bit, on):
+    return position + on * (bit - 2 * bit * lax.rem(position // bit, 2))
+
+
+def spread(pack, cot, index, local):
+    micros, own_rows, width = cot.shape
+    columns = pack.shape[1]
+    anywhere = pl.BlockSpec(memory_space=pl.ANY)
+    vector = pl.BlockSpec(memory_space=pltpu.VMEM)
+    dma = pltpu.SemaphoreType.DMA
+    return pl.pallas_call(
+        functools.partial(spread_kernel, local),
+        in_specs=[anywhere, vector, vector],
+        out_specs=[vector] * 4 + [anywhere],
+        out_shape=[
+            jax.ShapeDtypeStruct((2, 4, width, columns), jnp.bfloat16),
+            jax.ShapeDtypeStruct((8, width), jnp.float32),
+            jax.ShapeDtypeStruct((LANES, width), jnp.bfloat16),
+            jax.ShapeDtypeStruct((LANES, width), jnp.float32),
+            jax.ShapeDtypeStruct((local, micros * 8 * CAP, width), jnp.bfloat16),
+        ],
+        scratch_shapes=[
+            pltpu.VMEM((32,) + pack.shape, jnp.bfloat16),
+            pltpu.VMEM((32, width // 32, LANES), jnp.float32),
+            pltpu.VMEM((micros, 2, own_rows, width), jnp.bfloat16),
+            pltpu.VMEM((micros, 8, local, CAP, width), jnp.bfloat16),
+            dma, dma((5,)), dma((5,)), dma((micros,)), dma((micros,)),
+            dma((micros, 8, local)), dma((micros, 8, local)), dma((micros, local)),
+        ],
+        compiler_params=pltpu.CompilerParams(vmem_limit_bytes=VMEM, has_side_effects=True),
+        cost_estimate=pl.CostEstimate(flops=1000, bytes_accessed=1000, transcendentals=0),
+        name="spread",
+    )(pack, cot, index)
+
+
+def front_kernel(
+    local, per_step, tok_ref, bias_ref, mats_ref, norms_ref, parts_ref, index_ref,
+    middle_ref, proj_ref, mixed_ref, gates_ref, slots_ref,
+    shared, staged, pair_send, pair_recv, slot_send, slot_recv, slot_keep,
+):
+    at_t = lax.axis_index("t")
+    images, length, width = tok_ref.shape
+    micros, _, own_rows, _ = shared.shape
+    rows = per_step * length
+    steps = own_rows // rows
+
+    def swap(m, s):
+        here = pl.ds(pl.multiple_of(s * rows, 16), rows)
+        return to_peer(shared.at[m, 0, here], shared.at[m, 1, here], pair_send.at[m, s],
+                       pair_recv.at[m, s], {"t": 1 - at_t})
+
+    def attend(n, carry):
+        m, s = n // steps, lax.rem(n, steps)
+        _, low = forward_rows(n * per_step, per_step, tok_ref, bias_ref, mats_ref, norms_ref, parts_ref,
+                              middle_ref, proj_ref, mixed_ref, gates_ref)
+        shared[m, 0, pl.ds(pl.multiple_of(s * rows, 16), rows)] = low
+        swap(m, s).start()
+        return carry
+
+    lax.fori_loop(0, micros * steps, attend, 0)
+    plan = Dispatch(index_ref, shared, staged, slots_ref, slot_send, slot_recv, slot_keep, 8, 2, local)
+    for m in range(micros):
+        for s in range(steps):
+            swap(m, s).wait()
+        plan.send(m)
+    for m in range(micros):
+        plan.finish(m)
+
+
+def front(tok, bias, mats, norms, parts, index, local, per_step):
+    images, length, width = tok.shape
+    micros, _, _, own_rows = index.shape
+    steps = own_rows // (per_step * length)
+    anywhere = pl.BlockSpec(memory_space=pl.ANY)
+    vector = pl.BlockSpec(memory_space=pltpu.VMEM)
+    dma = pltpu.SemaphoreType.DMA
+    shapes = [(width, jnp.float32), (3 * width, jnp.bfloat16), (width, jnp.bfloat16), (LANES, jnp.float32)]
+    return pl.pallas_call(
+        functools.partial(front_kernel, local, per_step),
+        in_specs=[vector] * 6,
+        out_specs=[vector] * 4 + [anywhere],
+        out_shape=[jax.ShapeDtypeStruct((images, length, n), kind) for n, kind in shapes] + [
+            jax.ShapeDtypeStruct((local, micros * 8 * CAP, width), jnp.bfloat16)],
+        scratch_shapes=[
+            pltpu.VMEM((micros, 2, own_rows, width), jnp.bfloat16),
+            pltpu.VMEM((micros, 8, local, CAP, width), jnp.bfloat16),
+            dma((micros, steps)), dma((micros, steps)),
+            dma((micros, 8, local)), dma((micros, 8, local)), dma((micros, local)),
+        ],
+        compiler_params=pltpu.CompilerParams(vmem_limit_bytes=VMEM, has_side_effects=True),
+        cost_estimate=pl.CostEstimate(flops=1000, bytes_accessed=1000, transcendentals=0),
+        name="front",
+    )(tok, bias, mats, norms, parts, index)
+
+
 def per_device(planes, inner, parts, tokens, key_mask, expert_ids, slot_ids, norm1_gain, norm1_bias,
                qkv_weight, out_weight, norm2_gain, norm2_bias, router_weight, expert_in, expert_out,
                cotangent):
@@ -408,7 +660,7 @@
     gathered = lax.all_gather(packed, ("o", "i"), axis=0)
     gathered = lax.all_gather(gathered, "t", axis=0)
     mats = gathered[:, :, :4 * depth].reshape(parts, planes * inner, 4, depth, columns)
-    mats = mats.transpose(2, 1, 3, 0, 4).reshape(4, width, width)
+    mats = mats.transpose(2, 1, 3, 0, 4).reshape(1, 4, width, width)
     loose_all = gathered[:, :, 4 * depth:].reshape(parts, planes * inner, loose_rows * columns)
     loose_all = loose_all[:, :, :loose_count].astype(jnp.float32)
     loose_all = loose_all.reshape(parts, planes * inner, 3, small, 4 + experts)
@@ -416,7 +668,8 @@
     loose_all = loose_all.transpose(1, 0, 2, 3).reshape(width, 4 + experts)
     norms = loose_all[:, :4].T
     router = jnp.pad(loose_all[:, 4:], ((0, 0), (0, LANES - experts)))
-    router_three = jnp.stack(three_parts(router))
+    router_parts = jnp.concatenate(three_parts(router[:, :experts]), 1).T
+    router_parts = jnp.pad(router_parts, ((0, LANES - 3 * experts), (0, 0)))
 
     weights = []
     first_in = expert_in.reshape(homes, local, depth, extent)
@@ -467,14 +720,14 @@
     bias = jnp.where(flags > 0, 0.0, -1e30).astype(jnp.float32)
     tok = tokens.reshape(total, length, width)
     per_step = 2 if total % 2 == 0 else 1
-    middle, routed, proj, mixed, gates = attention_forward(tok, bias, mats, norms, router, per_step)
+    middle, routed, proj, mixed, gates = attention_forward(tok, bias, mats, norms, router_parts, per_step)
 
     row_slots = dispatch(share(routed.reshape(micros, own_rows, width)))
 
     first_out, second_out, results, backs = [], [], [], []
     for k in range(local):
         expert = ((inner_at * parts + part_at) * local + k).astype(jnp.int32).reshape(1)
-        result, back, dweights = run_expert(expert, row_slots[k], cot_slots[k], weights[k], router_three)
+        result, back, dweights = run_expert(expert, row_slots[k], cot_slots[k], weights[k], router_parts)
         results.append(result.reshape(micros, inner, CAP, width))
         backs.append(back.reshape(micros, inner, CAP, width + LANES))
         dweights = dweights.reshape(planes, homes, 2, depth, extent)
@@ -545,6 +798,124 @@
     )
 
 
+def per_device_halves(tokens, key_mask, expert_ids, slot_ids, norm1_gain, norm1_bias,
+                      qkv_weight, out_weight, norm2_gain, norm2_bias, router_weight, expert_in, expert_out,
+                      cotangent):
+    micros, own_rows, width = tokens.shape
+    length = key_mask.shape[2]
+    images = own_rows // length
+    total = micros * images
+    planes, inner, parts = 2, 8, 2
+    experts = expert_in.shape[0]
+    homes = inner * parts
+    local = experts // homes
+    depth, extent = expert_in.shape[1:]
+    columns = qkv_weight.shape[2]
+    plane_at, inner_at, part_at = (lax.axis_index(name) for name in ("o", "i", "t"))
+    low = jnp.bfloat16
+    across = [(0, 1), (1, 0)]
+
+    first_in = expert_in.reshape(homes, local, depth, extent)
+    second_in = expert_out.transpose(0, 2, 1).reshape(homes, local, depth, extent)
+    weights = []
+    for k in range(local):
+        both = jnp.stack([first_in[:, k], second_in[:, k]], 1)
+        mine = lax.all_to_all(both, ("i", "t"), 0, 0, tiled=True)
+        other = lax.ppermute(mine, "o", across)
+        full = jnp.where(plane_at == 0, jnp.stack([mine, other]), jnp.stack([other, mine]))
+        weights.append(full.reshape(planes, inner, parts, 2, depth, extent))
+
+    norms_in = jnp.stack([norm1_gain, norm1_bias, norm2_gain, norm2_bias], 1)
+    loose = [p for p in three_parts(router_weight)]
+    loose += [jnp.pad(p, ((0, 0), (0, 4))) for p in three_parts(norms_in)]
+    loose = jnp.concatenate(loose, 1)
+    loose = jnp.pad(loose, ((0, 0), (0, columns - loose.shape[1])))
+    packed = jnp.concatenate([
+        qkv_weight.transpose(1, 0, 2).reshape(3 * depth, columns), out_weight.T, loose], 0)
+    slot_index = jnp.where(slot_ids >= 0, expert_ids * CAP + slot_ids, -1).transpose(0, 2, 1)
+    own_first = part_at * own_rows
+    index = jnp.stack([
+        lax.dynamic_slice_in_dim(slot_index, own_first, own_rows, 2),
+        lax.dynamic_slice_in_dim(slot_index, own_rows - own_first, own_rows, 2)], 2)
+    mats, norms, router_parts, router_t, cot_slots = spread(packed, cotangent, index, local)
+
+    flags = lax.dynamic_slice_in_dim(key_mask, part_at * images, images, 1).reshape(total, 1, length)
+    bias = jnp.where(flags > 0, 0.0, -1e30).astype(jnp.float32)
+    tok = tokens.reshape(total, length, width)
+    middle, proj, mixed, gates, row_slots = front(tok, bias, mats, norms, router_parts, index, local, 2)
+
+    results, backs, finals = [], [], []
+    for k in range(local):
+        expert = ((inner_at * parts + part_at) * local + k).astype(jnp.int32).reshape(1)
+        result, back, dweights = run_expert(expert, row_slots[k], cot_slots[k], weights[k], router_parts)
+        results.append(result.reshape(micros, inner, CAP, width))
+        backs.append(back.reshape(micros, inner, CAP, width + LANES))
+        dweights = dweights.reshape(planes, homes, 2, depth, extent)
+        theirs = lax.dynamic_index_in_dim(dweights, 1 - plane_at, 0, keepdims=False)
+        ours = lax.dynamic_index_in_dim(dweights, plane_at, 0, keepdims=False)
+        summed = ours.astype(jnp.float32) + lax.ppermute(theirs, "o", across).astype(jnp.float32)
+        finals.append(lax.all_to_all(summed.astype(low), ("i", "t"), 0, 0, tiled=True))
+    first_grad = jnp.stack([f[:, 0] for f in finals], 1).reshape(experts, depth, extent)
+    second_grad = jnp.stack([f[:, 1] for f in finals], 1).reshape(experts, depth, extent)
+    first_grad = first_grad.astype(jnp.float32)
+    second_grad = second_grad.astype(jnp.float32).transpose(0, 2, 1)
+
+    homes_i = lax.broadcasted_iota(jnp.int32, (inner, local, CAP), 0)
+    locals_i = lax.broadcasted_iota(jnp.int32, (inner, local, CAP), 1)
+    cap_i = lax.broadcasted_iota(jnp.int32, (inner, local, CAP), 2)
+    places = (((homes_i * parts + part_at) * local + locals_i) * CAP + cap_i).reshape(1, -1)
+
+    def table(m, half):
+        first, second = index[m, 0, half][:, None], index[m, 1, half][:, None]
+        return ((first == places) | (second == places)).astype(low)
+
+    def collect(values):
+        size = values[0].shape[-1]
+        answers = []
+        for m in range(micros):
+            back = jnp.stack([v[m] for v in values], 1).reshape(inner, local * CAP, size)
+            back = lax.all_to_all(back, "i", 0, 0, tiled=True).reshape(inner * local * CAP, size)
+            away = mm(table(m, 1), back).astype(low)
+            here = mm(table(m, 0), back)
+            answers.append(here + lax.ppermute(away, "t", across).astype(jnp.float32))
+        return jnp.stack(answers)
+
+    grad = collect(backs)
+    combined = collect(results)
+    block_out = middle.reshape(micros, own_rows, width) + combined
+
+    input_grad, dmats, dnorms, drouter = attention_backward(
+        tok, middle, cotangent.reshape(total, length, width), grad.reshape(total, length, width + LANES),
+        gates, proj, mixed, bias, mats, norms, router_t, 2)
+    input_grad = input_grad.reshape(micros, own_rows, width)
+
+    small = norm1_gain.shape[0]
+    loose_count = 3 * small * (4 + experts)
+    loose_rows = -(-loose_count // (16 * columns)) * 16
+    dmats = dmats.reshape(parts, 4, planes, inner, depth, columns).transpose(3, 0, 2, 1, 4, 5)
+    dmats = dmats.reshape(homes, planes, 4 * depth, columns)
+    dloose = jnp.concatenate([dnorms.T, drouter[:, :experts]], 1)
+    dloose = dloose.reshape(planes, inner, parts, small * (4 + experts)).transpose(1, 2, 0, 3)
+    dloose = jnp.concatenate(three_parts(dloose), -1)
+    dloose = jnp.pad(dloose, ((0, 0),) * 3 + ((0, loose_rows * columns - loose_count),))
+    dloose = dloose.reshape(homes, planes, loose_rows, columns)
+    payload = jnp.concatenate([dmats, dloose], 2)
+    payload = lax.all_to_all(payload, ("i", "t"), 0, 0, tiled=True)
+    payload = jnp.sum(payload.astype(jnp.float32), 0)
+    theirs = lax.dynamic_index_in_dim(payload, 1 - plane_at, 0, keepdims=False)
+    ours = lax.dynamic_index_in_dim(payload, plane_at, 0, keepdims=False)
+    reduced = ours + lax.ppermute(theirs, "o", across)
+    matrices = reduced[:4 * depth].reshape(4, depth, columns)
+    qkv_grad = matrices[:3].transpose(1, 0, 2)
+    out_grad = matrices[3].T
+    tail = reduced[4 * depth:].reshape(-1)[:loose_count].reshape(3, small, 4 + experts)
+    tail = (tail[0] + tail[1]) + tail[2]
+    return (
+        block_out, input_grad, tail[:, 0], tail[:, 1], qkv_grad, out_grad, tail[:, 2], tail[:, 3],
+        tail[:, 4:], first_grad, second_grad,
+    )
+
+
 def solution(mesh):
     dp, parts = mesh.shape["dp"], mesh.shape["tensor"]
     inner = min(8, 32 // parts, dp)
@@ -553,8 +924,11 @@
     dps = ("o", "i")
     every = ("o", "i", "t")
     rows = P(None, every, None)
+    step = functools.partial(per_device, planes, inner, parts)
+    if (planes, inner, parts) == (2, 8, 2):
+        step = per_device_halves
     return jax.shard_map(
-        functools.partial(per_device, planes, inner, parts),
+        step,
         mesh=fine,
         in_specs=(
             rows, P(None, dps, None), P(None, dps, None), P(None, dps, None), P(every), P(every),

time: 1100 us -> 962 us (0.87)
  waiting for transfers between devices: 672 us -> 407 us
  Pallas kernels: 159 us -> 378 us
  matrix products: 61.2 us -> 32.9 us
  starting transfers between devices: 79.3 us -> 57.4 us
  local copies, waits for them, and re-layouts: 52.9 us -> 35.2 us
  between operations: 14.9 us -> 1.38 us
    pallas_call x1 -> x2, Pallas kernels: 23.7 us -> 245 us  [the longest x1 162 us: spread(): pl.pallas_call(functools.partial(spread_kernel, local), in_specs=[anywher...]
    ppermute x11 -> x9, waiting for transfers between devices: 531 us -> 313 us  [the longest x2 178 us: per_device_halves(): lax.ppermute(theirs, 'o', across).astype(jnp.float32)]
    all_gather x2 -> x0, waiting for transfers between devices: 30.1 us -> none  [the longest x1 30 us: per_device(): gathered = lax.all_gather(gathered, 't', axis=0)]
    dot_general x12 -> x8, matrix products: 61.2 us -> 32.9 us  [mm(): lax.dot_general(a, b, dims, precision=precision, preferred_element_type=j...]
    all_to_all x9 -> x5, starting transfers between devices: 43.3 us -> 23.9 us  [the longest x2 10.6 us: per_device_halves(): mine = lax.all_to_all(both, ('i', 't'), 0, 0, tiled=True)]
    all_to_all x9 -> x5, waiting for transfers between devices: 41.2 us -> 24.2 us  [the longest x2 24.1 us: per_device_halves(): mine = lax.all_to_all(both, ('i', 't'), 0, 0, tiled=True)]
  transfers between devices with their start and end apart: 26 -> 18, of which waited for: 16 -> 11; matrix products, arithmetic and copies ran while one was open for 13% -> 10% of each run, Pallas kernels for 7% -> 35%
where the time goes in v2:
time: 962 us; the launch traced here: 957 us
  waiting for transfers between devices  407 us (42%)
  Pallas kernels  378 us (39%)
  starting transfers between devices  57.4 us (6%)
  other arithmetic  45.7 us (5%)
  local copies, waits for them, and re-layouts  35.2 us (4%)
  matrix products  32.9 us (3%)
    ppermute x2, waiting for transfers between devices, per_device_halves(): lax.ppermute(theirs, 'o', across).astype(jnp.float32)  178 us
    pallas_call x1, Pallas kernels, spread(): pl.pallas_call(functools.partial(spread_kernel, local), in_specs=[anywher...  162 us
    ppermute x4, waiting for transfers between devices, collect(): answers.append(here + lax.ppermute(away, 't', across).astype(jnp.float32))  89.3 us
    pallas_call x2, Pallas kernels, run_expert(): pl.pallas_call(expert_kernel, grid_spec=pltpu.PrefetchScalarGridSpec(num_...  84.7 us
    pallas_call x1, Pallas kernels, front(): pl.pallas_call(functools.partial(front_kernel, local, per_step), in_specs...  82.2 us
    all_to_all x4, waiting for transfers between devices, collect(): lax.all_to_all(back, 'i', 0, 0, tiled=True)  69.4 us
    pallas_call x1, Pallas kernels, attention_backward(): pl.pallas_call(backward_kernel, grid=(images // per_step,), in_specs=[row...  48.8 us
    ppermute x2, waiting for transfers between devices, per_device_halves(): other = lax.ppermute(mine, 'o', across)  41 us
  transfers between devices with their start and end apart: 18, of which 11 were waited for; matrix products, arithmetic and copies ran while one was open for 10% of the time, Pallas kernels for 35%

profile of v2, /device:TPU:4, one launch (start us, length us, event | category | flops | bytes accessed | tf_op | source)
XLA Modules:
  0.0 957.5 jit_solution(7129173075864900320)
XLA Ops:
  6.0 5.3 all-to-all-start
  14.1 24.1 %all-to-all-done = bf16[16,2,32,1024]{3,2,1,0:T(8,128)(2,1)S(1)} async-done(((bf16[16,2,32,1024]{3,2,1,0:T(8,128)(2,1)}), bf16[16,2,32,1024]{3,2,1,0:T(8,128)(2,1)S(1)}, u32[]{:S(2)}, u32[]{:S(2)}) %all-to-all-start) | async-done | bytes 2097184 | tf_op jit(solution)/shard_map/all_to_all | solution.py:823
  39.6 5.3 all-to-all-start.1
  49.4 162.3 %spread.1 = (bf16[2,4,512,256]{3,2,1,0:T(8,128)(2,1)}, f32[8,512]{1,0:T(8,128)}, bf16[128,512]{1,0:T(8,128)(2,1)}, f32[128,512]{1,0:T(8,128)}, bf16[2,1920,512]{2,1,0:T(8,128)(2,1)}) custom-call(bf16[144,256]{1,0:T(8,128)(2,1)} %fusion.39.pack_ref, f32[2,800,512]{2,1,0:T(8,128)} %cot_ref.1, s32[2,2,2,800]{3,2,1,0:T(2,128)} %pad_add_fusion.index_ref), custom_call_target="tpu_custom_call" | custom-call | flops 1000 | bytes 1000 | tf_op jit(solution)/shard_map/spread/pallas_call | solution.py:549
  212.4 82.2 %front.1 = (f32[8,200,512]{2,1,0:T(8,128)}, bf16[8,200,1536]{2,1,0:T(8,128)(2,1)}, bf16[8,200,512]{2,1,0:T(8,128)(2,1)}, f32[8,200,128]{2,1,0:T(8,128)}, bf16[2,1920,512]{2,1,0:T(8,128)(2,1)}) custom-call(f32[8,200,512]{2,1,0:T(8,128)} %bitcast.157, f32[8,1,200]{2,1,0:T(1,128)} %select_n.47.bias_ref, bf16[2,4,512,256]{3,2,1,0:T(8,128)(2,1)} %get-tuple-element.31.mats_ref, ...), custom_call_target="tpu_custom_call" | custom-call | flops 1000 | bytes 1000 | tf_op jit(solution)/shard_map/front/pallas_call | solution.py:616
  294.7 5.7 slice_bitcast_fusion.2
  302.9 5.8 maximum_select_fusion.weights_ref
  308.7 42.3 %expert.2 = (bf16[1920,512]{1,0:T(8,128)(2,1)}, bf16[1920,640]{1,0:T(8,128)(2,1)}, bf16[2,8,2,2,32,1024]{5,4,3,2,1,0:T(8,128)(2,1)}) custom-call(s32[1]{0:T(128)} %bitcast.13.expert_ref, bf16[1920,512]{1,0:T(8,128)(2,1)} %get-tuple-element.95.slots_ref, bf16[1920,512]{1,0:T(8,128)(2,1)} %get-tuple-element.63.cots_ref, ...), custom_call_target="tpu_custom_call" | custom-call | flops 24159191040 | bytes 16252928 | tf_op jit(solution)/shard_map/expert/pallas_call | solution.py:371
  353.6 41.0 %collective-permute-done.1 = bf16[16,2,32,1024]{3,2,1,0:T(8,128)(2,1)} collective-permute-done((bf16[16,2,32,1024]{3,2,1,0:T(8,128)(2,1)S(1)}, bf16[16,2,32,1024]{3,2,1,0:T(8,128)(2,1)}, u32[]{:S(2)}, u32[]{:S(2)}) %collective-permute-start.1) | collective-permute-done | bytes 2097184 | tf_op jit(solution)/shard_map/ppermute | solution.py:824
  394.7 4.4 maximum_select_fusion.1.weights_ref
  399.1 42.4 %expert.3 = (bf16[1920,512]{1,0:T(8,128)(2,1)}, bf16[1920,640]{1,0:T(8,128)(2,1)}, bf16[2,8,2,2,32,1024]{5,4,3,2,1,0:T(8,128)(2,1)}) custom-call(s32[1]{0:T(128)} %bitcast.23.expert_ref, bf16[1920,512]{1,0:T(8,128)(2,1)} %get-tuple-element.94.slots_ref, bf16[1920,512]{1,0:T(8,128)(2,1)} %get-tuple-element.64.cots_ref, ...), custom_call_target="tpu_custom_call" | custom-call | flops 24159191040 | bytes 16252928 | tf_op jit(solution)/shard_map/expert/pallas_call | solution.py:371
  444.8 5.2 all-to-all-start.2
  451.4 22.4 %all-to-all-done.2 = bf16[8,240,512]{2,1,0:T(8,128)(2,1)} async-done(((bf16[8,240,512]{2,1,0:T(8,128)(2,1)}), bf16[8,240,512]{2,1,0:T(8,128)(2,1)}, u32[]{:S(2)}, u32[]{:S(2)}) %all-to-all-start.2) | async-done | bytes 1966112 | tf_op jit(solution)/shard_map/all_to_all | solution.py:877
  473.8 4.8 all-to-all-start.3
  482.9 19.5 %all-to-all-done.3 = bf16[8,240,512]{2,1,0:T(8,128)(2,1)} async-done(((bf16[8,240,512]{2,1,0:T(8,128)(2,1)}), bf16[8,240,512]{2,1,0:T(8,128)(2,1)}, u32[]{:S(2)}, u32[]{:S(2)}) %all-to-all-start.3) | async-done | bytes 1966112 | tf_op jit(solution)/shard_map/all_to_all | solution.py:877
  502.5 4.8 all-to-all-start.4
  509.0 27.5 %all-to-all-done.4 = bf16[8,240,640]{2,1,0:T(8,128)(2,1)} async-done(((bf16[8,240,640]{2,1,0:T(8,128)(2,1)}), bf16[8,240,640]{2,1,0:T(8,128)(2,1)}, u32[]{:S(2)}, u32[]{:S(2)}) %all-to-all-start.4) | async-done | bytes 2457632 | tf_op jit(solution)/shard_map/all_to_all | solution.py:877
  536.4 4.1 all-to-all-start.5
  544.7 92.8 %collective-permute-done.7 = bf16[16,2,32,1024]{3,2,1,0:T(8,128)(2,1)} collective-permute-done((bf16[16,2,32,1024]{3,2,1,0:T(8,128)(2,1)}, bf16[16,2,32,1024]{3,2,1,0:T(8,128)(2,1)}, u32[]{:S(2)}, u32[]{:S(2)}) %collective-permute-start.7) | collective-permute-done | bytes 2097184 | tf_op jit(solution)/shard_map/ppermute | solution.py:856
  637.6 4.6 fusion.9
  643.6 3.9 all-to-all-start.7
  652.3 5.8 fusion.35
  659.6 85.0 %collective-permute-done.8 = bf16[16,2,32,1024]{3,2,1,0:T(8,128)(2,1)} collective-permute-done((bf16[16,2,32,1024]{3,2,1,0:T(8,128)(2,1)}, bf16[16,2,32,1024]{3,2,1,0:T(8,128)(2,1)}, u32[]{:S(2)}, u32[]{:S(2)}) %collective-permute-start.8) | collective-permute-done | bytes 2097184 | tf_op jit(solution)/shard_map/ppermute | solution.py:856
  749.9 5.1 all-to-all-start.8
  755.0 4.6 fusion.34
  761.2 5.0 add_bitcast_fusion.1
  766.1 37.6 %collective-permute-done.5 = bf16[800,640]{1,0:T(8,128)(2,1)S(1)} collective-permute-done((bf16[800,640]{1,0:T(8,128)(2,1)S(1)}, bf16[800,640]{1,0:T(8,128)(2,1)S(1)}, u32[]{:S(2)}, u32[]{:S(2)}) %collective-permute-start.5) | collective-permute-done | bytes 1024032 | tf_op jit(solution)/shard_map/ppermute | solution.py:880
  808.9 48.8 %attention_backward.1 = (f32[8,200,512]{2,1,0:T(8,128)}, bf16[2,4,512,256]{3,2,1,0:T(8,128)(2,1)}, f32[4,512]{1,0:T(4,128)}, f32[512,128]{1,0:T(8,128)}) custom-call(f32[8,200,512]{2,1,0:T(8,128)} %bitcast.158, f32[8,200,512]{2,1,0:T(8,128)} %get-tuple-element.34.middle_ref, f32[8,200,512]{2,1,0:T(8,128)} %bitcast.156, f32[8,200,640]{2,1,0:T(8,128)} %bitcast.151, ...), custom_call_target="tpu_custom_call" | custom-call | flops 12582912000 | bytes 24576000 | tf_op jit(solution)/shard_map/attention_backward/pallas_call | solution.py:259
  862.7 4.3 all-to-all-start.6
  876.8 38.2 %collective-permute-done.2 = bf16[800,512]{1,0:T(8,128)(2,1)S(1)} collective-permute-done((bf16[800,512]{1,0:T(8,128)(2,1)S(1)}, bf16[800,512]{1,0:T(8,128)(2,1)S(1)}, u32[]{:S(2)}, u32[]{:S(2)}) %collective-permute-start.2) | collective-permute-done | bytes 819232 | tf_op jit(solution)/shard_map/ppermute | solution.py:880
  918.5 13.6 %collective-permute-done.3 = bf16[800,512]{1,0:T(8,128)(2,1)S(1)} collective-permute-done((bf16[800,512]{1,0:T(8,128)(2,1)S(1)}, bf16[800,512]{1,0:T(8,128)(2,1)S(1)}, u32[]{:S(2)}, u32[]{:S(2)}) %collective-permute-start.3) | collective-permute-done | bytes 819232 | tf_op jit(solution)/shard_map/ppermute | solution.py:880
  949.5 4.9 collective-permute-done.6
  (129 shorter events, 92.7 us)
Async XLA Ops:
  6.0 32.2 %all-to-all-start = ((bf16[16,2,32,1024]{3,2,1,0:T(8,128)(2,1)}), bf16[16,2,32,1024]{3,2,1,0:T(8,128)(2,1)S(1)}, u32[]{:S(2)}, u32[]{:S(2)}) async-start(bf16[16,2,32,1024]{3,2,1,0:T(8,128)(2,1)} %pad_maximum_fusion.4), calls=%async_computation | async-start | bytes 4194304 | tf_op jit(solution)/shard_map/all_to_all | solution.py:823
  14.0 33.5 %copy-start.12 = (s32[2,1600,2]{1,2,0:T(2,128)S(1)}, s32[2,1600,2]{1,2,0:T(2,128)}, u32[]{:S(2)}) copy-start(s32[2,1600,2]{1,2,0:T(2,128)} %param.17) | copy-start | bytes 76804
  14.0 33.5 %copy-start.13 = (s32[2,1600,2]{1,2,0:T(2,128)S(1)}, s32[2,1600,2]{1,2,0:T(2,128)}, u32[]{:S(2)}) copy-start(s32[2,1600,2]{1,2,0:T(2,128)} %param.16) | copy-start | bytes 76804
  14.0 33.7 %copy-start.17 = (f32[16]{0:T(128)S(1)}, f32[16]{0:T(128)}, u32[]{:S(2)}) copy-start(f32[16]{0:T(128)} %param.23) | copy-start | bytes 196
  14.0 33.7 %copy-start.18 = (f32[16]{0:T(128)S(1)}, f32[16]{0:T(128)}, u32[]{:S(2)}) copy-start(f32[16]{0:T(128)} %param.22) | copy-start | bytes 196
  14.0 33.7 %copy-start.19 = (f32[16]{0:T(128)S(1)}, f32[16]{0:T(128)}, u32[]{:S(2)}) copy-start(f32[16]{0:T(128)} %param.19) | copy-start | bytes 196
  14.0 33.7 %copy-start.20 = (f32[16]{0:T(128)S(1)}, f32[16]{0:T(128)}, u32[]{:S(2)}) copy-start(f32[16]{0:T(128)} %param.18) | copy-start | bytes 196
  14.1 34.0 %copy-start.15 = (f32[16,32]{1,0:T(8,128)S(1)}, f32[16,32]{1,0:T(8,128)}, u32[]{:S(2)}) copy-start(f32[16,32]{1,0:T(8,128)} %param.24) | copy-start | bytes 6148
  14.1 34.7 %copy-start.11 = (bf16[32,3,256]{2,0,1:T(8,128)(2,1)S(1)}, bf16[32,3,256]{2,0,1:T(8,128)(2,1)}, u32[]{:S(2)}) copy-start(bf16[32,3,256]{2,0,1:T(8,128)(2,1)} %param.20) | copy-start | bytes 147460
  14.1 34.7 %copy-start.14 = (bf16[256,32]{0,1:T(8,128)(2,1)S(1)}, bf16[256,32]{0,1:T(8,128)(2,1)}, u32[]{:S(2)}) copy-start(bf16[256,32]{0,1:T(8,128)(2,1)} %param.21) | copy-start | bytes 49156
  39.6 260.8 %all-to-all-start.1 = ((bf16[16,2,32,1024]{3,2,1,0:T(8,128)(2,1)}), bf16[16,2,32,1024]{3,2,1,0:T(8,128)(2,1)S(1)}, u32[]{:S(2)}, u32[]{:S(2)}) async-start(bf16[16,2,32,1024]{3,2,1,0:T(8,128)(2,1)} %pad_maximum_fusion.5), calls=%async_computation.1 | async-start | bytes 4194304 | tf_op jit(solution)/shard_map/all_to_all | solution.py:823
  44.9 166.9 %copy-start.16 = (s32[2,8,200]{2,1,0:T(8,128)S(1)}, s32[2,8,200]{2,1,0:T(8,128)}, u32[]{:S(2)}) copy-start(s32[2,8,200]{2,1,0:T(8,128)} %param.15) | copy-start | bytes 38404
  44.9 258.0 %collective-permute-start = (bf16[16,2,32,1024]{3,2,1,0:T(8,128)(2,1)}, bf16[16,2,32,1024]{3,2,1,0:T(8,128)(2,1)}, u32[]{:S(2)}, u32[]{:S(2)}) collective-permute-start(bf16[16,2,32,1024]{3,2,1,0:T(8,128)(2,1)} %copy-done.3), channel_id=1, source_target_pairs={{0,16},{16,0},{1,17},{17,1},{2,18},{18,2},{3,19},{19,3},{4,20},{20... | collective-permute-start | bytes 6291464 | tf_op jit(solution)/shard_map/ppermute | solution.py:824
  300.3 94.3 %collective-permute-start.1 = (bf16[16,2,32,1024]{3,2,1,0:T(8,128)(2,1)S(1)}, bf16[16,2,32,1024]{3,2,1,0:T(8,128)(2,1)}, u32[]{:S(2)}, u32[]{:S(2)}) collective-permute-start(bf16[16,2,32,1024]{3,2,1,0:T(8,128)(2,1)S(1)} %all-to-all-done.1), channel_id=1, source_target_pairs={{0,16},{16,0},{1,17},{17,1},{2,18},{18,2},{3,19},{19,3},{4,20},{20... | collective-permute-start | bytes 6291464 | tf_op jit(solution)/shard_map/ppermute | solution.py:824
  444.8 29.1 %all-to-all-start.2 = ((bf16[8,240,512]{2,1,0:T(8,128)(2,1)}), bf16[8,240,512]{2,1,0:T(8,128)(2,1)}, u32[]{:S(2)}, u32[]{:S(2)}) async-start(bf16[8,240,512]{2,1,0:T(8,128)(2,1)} %bitcast.31), calls=%async_computation.2 | async-start | bytes 3932160 | tf_op jit(solution)/shard_map/all_to_all | solution.py:877
  473.8 28.6 %all-to-all-start.3 = ((bf16[8,240,512]{2,1,0:T(8,128)(2,1)}), bf16[8,240,512]{2,1,0:T(8,128)(2,1)}, u32[]{:S(2)}, u32[]{:S(2)}) async-start(bf16[8,240,512]{2,1,0:T(8,128)(2,1)} %bitcast.38), calls=%async_computation.3 | async-start | bytes 3932160 | tf_op jit(solution)/shard_map/all_to_all | solution.py:877
  502.5 34.0 %all-to-all-start.4 = ((bf16[8,240,640]{2,1,0:T(8,128)(2,1)}), bf16[8,240,640]{2,1,0:T(8,128)(2,1)}, u32[]{:S(2)}, u32[]{:S(2)}) async-start(bf16[8,240,640]{2,1,0:T(8,128)(2,1)} %bitcast.46), calls=%async_computation.4 | async-start | bytes 4915200 | tf_op jit(solution)/shard_map/all_to_all | solution.py:877
  536.4 105.8 %all-to-all-start.5 = ((bf16[8,240,640]{2,1,0:T(8,128)(2,1)}), bf16[8,240,640]{2,1,0:T(8,128)(2,1)S(1)}, u32[]{:S(2)}, u32[]{:S(2)}) async-start(bf16[8,240,640]{2,1,0:T(8,128)(2,1)} %bitcast.53), calls=%async_computation.5 | async-start | bytes 4915200 | tf_op jit(solution)/shard_map/all_to_all | solution.py:877
  543.7 93.9 %collective-permute-start.7 = (bf16[16,2,32,1024]{3,2,1,0:T(8,128)(2,1)}, bf16[16,2,32,1024]{3,2,1,0:T(8,128)(2,1)}, u32[]{:S(2)}, u32[]{:S(2)}) collective-permute-start(bf16[16,2,32,1024]{3,2,1,0:T(8,128)(2,1)} %dynamic-slice_bitcast_fusion.1), channel_id=1, source_target_pairs={{0,16},{16,0},{1,17},{17,1},{2,18},{18,2},{3,19},{19,3},{4,20},{20... | collective-permute-start | bytes 6291464 | tf_op jit(solution)/shard_map/ppermute | solution.py:856
  643.6 104.8 %all-to-all-start.7 = ((bf16[16,2,32,1024]{3,2,1,0:T(8,128)(2,1)}), bf16[16,2,32,1024]{3,2,1,0:T(8,128)(2,1)S(1)}, u32[]{:S(2)}, u32[]{:S(2)}) async-start(bf16[16,2,32,1024]{3,2,1,0:T(8,128)(2,1)} %fusion.9), calls=%async_computation.7 | async-start | bytes 4194304 | tf_op jit(solution)/shard_map/all_to_all | solution.py:857
  650.7 93.9 %collective-permute-start.8 = (bf16[16,2,32,1024]{3,2,1,0:T(8,128)(2,1)}, bf16[16,2,32,1024]{3,2,1,0:T(8,128)(2,1)}, u32[]{:S(2)}, u32[]{:S(2)}) collective-permute-start(bf16[16,2,32,1024]{3,2,1,0:T(8,128)(2,1)} %dynamic-slice_bitcast_fusion), channel_id=1, source_target_pairs={{0,16},{16,0},{1,17},{17,1},{2,18},{18,2},{3,19},{19,3},{4,20},{20... | collective-permute-start | bytes 6291464 | tf_op jit(solution)/shard_map/ppermute | solution.py:856
  652.3 92.3 %copy-start.4 = (bf16[2,8,2,2,32,1024]{5,4,3,2,1,0:T(8,128)(2,1)S(1)}, bf16[2,8,2,2,32,1024]{5,4,3,2,1,0:T(8,128)(2,1)}, u32[]{:S(2)}) copy-start(bf16[2,8,2,2,32,1024]{5,4,3,2,1,0:T(8,128)(2,1)} %get-tuple-element.50) | copy-start | bytes 12582916
  658.1 103.0 %collective-permute-start.4 = (bf16[800,640]{1,0:T(8,128)(2,1)}, bf16[800,640]{1,0:T(8,128)(2,1)}, u32[]{:S(2)}, u32[]{:S(2)}) collective-permute-start(bf16[800,640]{1,0:T(8,128)(2,1)} %fusion.35), channel_id=1, source_target_pairs={{0,1},{1,0},{2,3},{3,2},{4,5},{5,4},{6,7},{7,6},{8,9},{9,8},{10,11... | collective-permute-start | bytes 3072008 | tf_op jit(solution)/shard_map/ppermute | solution.py:880
  749.9 112.8 %all-to-all-start.8 = ((bf16[16,2,32,1024]{3,2,1,0:T(8,128)(2,1)}), bf16[16,2,32,1024]{3,2,1,0:T(8,128)(2,1)}, u32[]{:S(2)}, u32[]{:S(2)}) async-start(bf16[16,2,32,1024]{3,2,1,0:T(8,128)(2,1)} %fusion.8), calls=%async_computation.8 | async-start | bytes 4194304 | tf_op jit(solution)/shard_map/all_to_all | solution.py:857
  759.6 44.2 %collective-permute-start.5 = (bf16[800,640]{1,0:T(8,128)(2,1)S(1)}, bf16[800,640]{1,0:T(8,128)(2,1)S(1)}, u32[]{:S(2)}, u32[]{:S(2)}) collective-permute-start(bf16[800,640]{1,0:T(8,128)(2,1)S(1)} %fusion.34), channel_id=1, source_target_pairs={{0,1},{1,0},{2,3},{3,2},{4,5},{5,4},{6,7},{7,6},{8,9},{9,8},{10,11... | collective-permute-start | bytes 3072008 | tf_op jit(solution)/shard_map/ppermute | solution.py:880
  761.1 42.6 %copy-start.8 = (bf16[8,240,640]{2,1,0:T(8,128)(2,1)S(1)}, bf16[8,240,640]{2,1,0:T(8,128)(2,1)}, u32[]{:S(2)}) copy-start(bf16[8,240,640]{2,1,0:T(8,128)(2,1)} %copy-done.7) | copy-start | bytes 7372804
  857.7 3.1 copy-start.10
  862.7 81.8 %all-to-all-start.6 = ((bf16[16,2,144,256]{3,2,1,0:T(8,128)(2,1)}), bf16[16,2,144,256]{3,2,1,0:T(8,128)(2,1)S(1)}, u32[]{:S(2)}, u32[]{:S(2)}) async-start(bf16[16,2,144,256]{3,2,1,0:T(8,128)(2,1)} %pad_maximum_fusion.3), calls=%async_computation.6 | async-start | bytes 4718592 | tf_op jit(solution)/shard_map/all_to_all | solution.py:903
  870.9 44.2 %collective-permute-start.2 = (bf16[800,512]{1,0:T(8,128)(2,1)S(1)}, bf16[800,512]{1,0:T(8,128)(2,1)S(1)}, u32[]{:S(2)}, u32[]{:S(2)}) collective-permute-start(bf16[800,512]{1,0:T(8,128)(2,1)S(1)} %fusion.37), channel_id=1, source_target_pairs={{0,1},{1,0},{2,3},{3,2},{4,5},{5,4},{6,7},{7,6},{8,9},{9,8},{10,11... | collective-permute-start | bytes 2457608 | tf_op jit(solution)/shard_map/ppermute | solution.py:880
  876.2 55.8 %collective-permute-start.3 = (bf16[800,512]{1,0:T(8,128)(2,1)S(1)}, bf16[800,512]{1,0:T(8,128)(2,1)S(1)}, u32[]{:S(2)}, u32[]{:S(2)}) collective-permute-start(bf16[800,512]{1,0:T(8,128)(2,1)S(1)} %fusion.36), channel_id=1, source_target_pairs={{0,1},{1,0},{2,3},{3,2},{4,5},{5,4},{6,7},{7,6},{8,9},{9,8},{10,11... | collective-permute-start | bytes 2457608 | tf_op jit(solution)/shard_map/ppermute | solution.py:880
  932.1 3.6 copy-start.6
  944.9 9.5 collective-permute-start.6
  (7 other events, 13.2 us)
